TPU v7x, 32 devices: a whole 2x2x4 slice. The times are simulated.
32 devices in a mesh: left: 8 (over y, x, core), right: 4 (over z).
Axes of the slice: x: 2, y: 2, z: 4, core: 2. Of those that a mesh axis runs over, the one named last changes fastest.
Arguments:
- tracer: float32 [2, 1024, 256, 128], P(None, None, 'left', 'right'), may hold values from -6 to 6
- symbol_x: float32 [1024], replicated, may hold values from 0.3 to 3
- symbol_y: float32 [256], replicated, may hold values from 0.3 to 3
- symbol_z: float32 [128], replicated, may hold values from 0.3 to 3
Outputs:
- modes: float32 [2, 1024, 256, 128], P(None, 'left', 'right')
All inputs are finite; a program needn't handle non-finite values.
Results may differ from a plain program's by a relative error of at most 0.00007.
Values sent between devices are 32-bit elements; how exact they have to be, the bound alone decides.
A program may use at most 256 MiB of HBM per device.

v0:
```python
import functools
import math

import jax
import jax.numpy as jnp
import numpy as np
from jax import lax
from jax.experimental import pallas as pl
from jax.experimental.pallas import tpu as pltpu
from jax.sharding import PartitionSpec as P

MESH = pl.DeviceIdType.MESH
NEAR_BYTES = 20 * 2**20
DEPTH = 8
BAND = 16
LANES = 128
SLOTS = 3


def transform_table(count):
    inner = 1 << ((count.bit_length() - 1) // 2)
    outer = count // inner
    column = np.arange(count)

    def angle(row):
        return 2.0 * np.pi / count * (row[:, None] * column[None, :] % count)

    low = angle(np.arange(inner))
    high = angle(np.arange(outer) * inner)
    scale = count ** (-0.5)
    cos_low = jnp.asarray(np.cos(low), jnp.float32)[None]
    sin_low = jnp.asarray(np.sin(low), jnp.float32)[None]
    plus = jnp.asarray((np.cos(high) + np.sin(high)) * scale, jnp.float32)[:, None]
    minus = jnp.asarray((np.cos(high) - np.sin(high)) * scale, jnp.float32)[:, None]
    return (cos_low * plus + sin_low * minus).reshape(count, count)


def halves_of(table):
    upper = lax.reduce_precision(table, 8, 7)
    return jnp.stack([upper.astype(jnp.bfloat16), (table - upper).astype(jnp.bfloat16)])


def small_table(count):
    rank = np.arange(count)
    angle = 2.0 * np.pi / count * (rank[:, None] * rank[None, :] % count)
    table = ((np.cos(angle) + np.sin(angle)) * count ** (-0.5)).astype(np.float32)
    upper = table.astype(jnp.bfloat16)
    return jnp.asarray(np.stack([upper, (table - upper.astype(np.float32)).astype(jnp.bfloat16)]))


def split(values):
    upper = values.astype(jnp.bfloat16)
    return upper, (values - upper.astype(jnp.float32)).astype(jnp.bfloat16)


def product(a, b):
    dot = functools.partial(jnp.dot, preferred_element_type=jnp.float32)
    return dot(a[0], b[0]) + (dot(a[0], b[1]) + dot(a[1], b[0]))


def landed(ref, sem):
    pltpu.make_async_copy(ref, ref, sem).wait()


def kernel(lefts, rights, near, data, hx, hy, hz, base, sym_y, out, *rest):
    (first, second, dbuf, lines, send_a, send_b, obuf,
     d_sem, sa_sem, ra_sem, y_sem, sb_sem, rb_sem, z_sem, o_sem, *staging) = rest
    fields, share_y, share_z, _ = data.shape
    size_y, size_z = hy.shape[1], hz.shape[1]
    share_x = base.shape[0]
    bands = out.shape[1]
    pieces = share_z // DEPTH
    chunks = fields * pieces
    rows = share_y * DEPTH
    flat = DEPTH * BAND
    out_y = bands * BAND
    left, right = lax.axis_index("left"), lax.axis_index("right")

    def load(i):
        source = data.at[i // pieces, :, pl.ds(lax.rem(i, pieces) * DEPTH, DEPTH), :]
        return pltpu.make_async_copy(source, dbuf.at[lax.rem(i, 2)], d_sem.at[lax.rem(i, 2)])

    load(0).start()

    barrier = pltpu.get_barrier_semaphore()
    for k in range(1, lefts):
        pl.semaphore_signal(barrier, inc=1, device_id=(lax.rem(left + k, lefts), right), device_id_type=MESH)
    for k in range(1, rights):
        pl.semaphore_signal(barrier, inc=1, device_id=(left, lax.rem(right + k, rights)), device_id_type=MESH)
    pl.semaphore_wait(barrier, lefts + rights - 2)

    def copy_a(i, to):
        slot = lax.rem(i, SLOTS)
        return pltpu.make_async_remote_copy(
            src_ref=send_a.at[slot, to],
            dst_ref=first.at[i, pl.ds(left * rows, rows)],
            send_sem=sa_sem.at[slot, to],
            recv_sem=ra_sem.at[i, left],
            device_id=(to, right),
            device_id_type=MESH,
        )

    def copy_b(i, to, band):
        spot = right * share_z + lax.rem(i, pieces) * DEPTH
        return pltpu.make_async_remote_copy(
            src_ref=send_b.at[i, to, band],
            dst_ref=second.at[i // pieces, band, pl.ds(spot * BAND, flat)],
            send_sem=sb_sem.at[i, to, band],
            recv_sem=rb_sem.at[i, right, band],
            device_id=(left, to),
            device_id_type=MESH,
        )

    def sent_a(i):
        for k in range(1, lefts):
            copy_a(i, lax.rem(left + k, lefts)).wait_send()

    def x_step(i):
        load(i).wait()

        @pl.when(i + 1 < chunks)
        def _():
            load(i + 1).start()

        @pl.when(i >= SLOTS)
        def _():
            sent_a(i - SLOTS)

        slot = lax.rem(i, SLOTS)
        lines[0], lines[1] = split(dbuf[lax.rem(i, 2)].reshape(rows, hx.shape[1]))

        def tile(j, carry):
            cols = pl.ds(pl.multiple_of(j * 2 * share_x, 2 * share_x), 2 * share_x)
            got = product((lines[0], lines[1]), (hx[0, :, cols], hx[1, :, cols]))
            send_a[slot, 2 * j] = got[:, :share_x]
            send_a[slot, 2 * j + 1] = got[:, share_x:]
            return carry

        lax.fori_loop(0, lefts // 2, tile, 0)
        for k in range(1, lefts):
            copy_a(i, lax.rem(left + k, lefts)).start()
        pltpu.make_async_copy(
            send_a.at[slot, left], first.at[i, pl.ds(left * rows, rows)], ra_sem.at[i, left]
        ).start()

    def y_step(i):
        for k in range(lefts):
            landed(first.at[i, pl.ds(k * rows, rows)], ra_sem.at[i, k])
        if near:
            block = first.at[i]
        else:
            block = staging[0]
            fetch = pltpu.make_async_copy(first.at[i], block, y_sem)
            fetch.start()
            fetch.wait()
        for z in range(0, DEPTH, 2):
            pair = jnp.concatenate(
                [block[pl.ds(z, size_y, stride=DEPTH), :], block[pl.ds(z + 1, size_y, stride=DEPTH), :]], axis=1
            )
            got = product((hy[0], hy[1]), split(pair))
            for to in range(rights):
                for band in range(bands):
                    top = to * out_y + band * BAND
                    for half in range(2):
                        send_b[i, to, band, (z + half) * BAND:(z + half + 1) * BAND, :] = (
                            got[top:top + BAND, half * share_x:(half + 1) * share_x]
                        )
        for band in range(bands):
            for k in range(rights):
                to = jnp.where(right < rights // 2, rights - 1 - k, k)

                @pl.when(to != right)
                def _():
                    copy_b(i, to, band).start()

            spot = right * share_z + lax.rem(i, pieces) * DEPTH
            pltpu.make_async_copy(
                send_b.at[i, right, band],
                second.at[i // pieces, band, pl.ds(spot * BAND, flat)],
                rb_sem.at[i, right, band],
            ).start()

    def step(i, carry):
        @pl.when(i < chunks)
        def _():
            x_step(i)

        @pl.when(i >= 1)
        def _():
            y_step(i - 1)

        return carry

    lax.fori_loop(0, chunks + 1, step, 0)

    def put(n):
        slot = lax.rem(n, 2)
        return pltpu.make_async_copy(obuf.at[slot], out.at[n // bands, lax.rem(n, bands)], o_sem.at[slot])

    def z_step(n, carry):
        field, band = n // bands, lax.rem(n, bands)
        slot = lax.rem(n, 2)

        def arrive(p, carry):
            for k in range(rights):
                spot = k * share_z + p * DEPTH
                landed(second.at[field, band, pl.ds(spot * BAND, flat)], rb_sem.at[field * pieces + p, k, band])
            return carry

        lax.fori_loop(0, pieces, arrive, 0)
        if near:
            block = second.at[field, band]
        else:
            block = staging[1]
            fetch = pltpu.make_async_copy(second.at[field, band], block, z_sem)
            fetch.start()
            fetch.wait()

        @pl.when(n >= 2)
        def _():
            put(n - 2).wait()

        def line(y, carry):
            plane = block[pl.ds(y, size_z, stride=BAND), :].T
            got = product(split(plane), (hz[0], hz[1]))
            got = got * lax.rsqrt(base[...] + sym_y[right * out_y + band * BAND + y])
            for t in range(size_z // LANES):
                obuf[slot, t, pl.ds(y, share_x, stride=BAND), :] = got[:, t * LANES:(t + 1) * LANES]
            return carry

        lax.fori_loop(0, BAND, line, 0, unroll=2)
        put(n).start()
        return carry

    steps = fields * bands
    lax.fori_loop(0, steps, z_step, 0)

    def drain_a(i, carry):
        sent_a(i)
        return carry

    lax.fori_loop(max(chunks - SLOTS, 0), chunks, drain_a, 0)

    def drain_b(i, carry):
        for k in range(1, rights):
            for band in range(bands):
                copy_b(i, lax.rem(right + k, rights), band).wait_send()
        return carry

    lax.fori_loop(0, chunks, drain_b, 0)
    for n in range(max(steps - 2, 0), steps):
        put(n).wait()


def local(lefts, rights, tracer, symbol_x, symbol_y, symbol_z):
    fields, size_x, share_y, share_z = tracer.shape
    size_y, size_z = symbol_y.shape[0], symbol_z.shape[0]
    share_x, out_y = size_x // lefts, size_y // rights
    bands = out_y // BAND
    chunks = fields * (share_z // DEPTH)
    data = jnp.transpose(tracer, (0, 2, 3, 1))
    part_x = lax.dynamic_slice_in_dim(symbol_x, lax.axis_index("left") * share_x, share_x)
    base = part_x[:, None] + symbol_z[None, :]
    f32 = jnp.float32
    any_space = pl.BlockSpec(memory_space=pl.ANY)
    vmem = pl.BlockSpec(memory_space=pltpu.VMEM)
    landing = [(chunks, size_y * DEPTH, share_x), (fields, bands, size_z * BAND, share_x)]
    near = 4 * sum(map(math.prod, landing)) <= NEAR_BYTES
    staging = [] if near else [
        pltpu.VMEM((size_y * DEPTH, share_x), f32), pltpu.VMEM((size_z * BAND, share_x), f32)
    ]
    results = pl.pallas_call(
        functools.partial(kernel, lefts, rights, near),
        name="modes",
        out_shape=[
            jax.ShapeDtypeStruct((fields, bands, size_z // LANES, share_x * BAND, LANES), f32),
            *([] if near else [jax.ShapeDtypeStruct(shape, f32) for shape in landing]),
        ],
        in_specs=[any_space, vmem, vmem, vmem, vmem, pl.BlockSpec(memory_space=pltpu.SMEM)],
        out_specs=[any_space] * (1 if near else 3),
        scratch_shapes=[
            *([pltpu.VMEM(shape, f32) for shape in landing] if near else []),
            pltpu.VMEM((2, share_y, DEPTH, size_x), f32),
            pltpu.VMEM((2, share_y * DEPTH, size_x), jnp.bfloat16),
            pltpu.VMEM((SLOTS, lefts, share_y * DEPTH, share_x), f32),
            pltpu.VMEM((chunks, rights, bands, DEPTH * BAND, share_x), f32),
            pltpu.VMEM((2, size_z // LANES, share_x * BAND, LANES), f32),
            pltpu.SemaphoreType.DMA((2,)),
            pltpu.SemaphoreType.DMA((SLOTS, lefts)),
            pltpu.SemaphoreType.DMA((chunks, lefts)),
            pltpu.SemaphoreType.DMA,
            pltpu.SemaphoreType.DMA((chunks, rights, bands)),
            pltpu.SemaphoreType.DMA((chunks, rights, bands)),
            pltpu.SemaphoreType.DMA,
            pltpu.SemaphoreType.DMA((2,)),
            *staging,
        ],
        compiler_params=pltpu.CompilerParams(
            collective_id=0, has_side_effects=True, vmem_limit_bytes=60 * 2**20
        ),
    )(data, halves_of(transform_table(size_x)), small_table(size_y), small_table(size_z), base, symbol_y)
    out = results[0].reshape(fields, bands, size_z // LANES, share_x, BAND, LANES)
    return jnp.transpose(out, (0, 3, 1, 4, 2, 5)).reshape(fields, share_x, out_y, size_z)


def solution(mesh):
    return jax.shard_map(
        functools.partial(local, mesh.shape["left"], mesh.shape["right"]),
        mesh=mesh,
        in_specs=(P(None, None, "left", "right"), P(), P(), P()),
        out_specs=P(None, "left", "right", None),
        check_vma=False,
    )
```

profile of v0, /device:TPU:0, one launch (start us, length us, event | category | flops | bytes accessed | tf_op | source)
XLA Modules:
  0.0 222.9 jit_solution(8860441879024706694)
XLA Ops:
  0.0 0.8 dynamic_slice.3
  0.8 1.4 broadcast_add_fusion.base
  2.1 1.7 multiply_add_fusion
  3.9 0.9 reduce-precision_convert_fusion
  4.8 2.4 %pad_maximum_fusion.hx = bf16[2,1024,1024]{2,1,0:T(8,128)(2,1)} fusion(bf16[1,1024,1024]{2,1,0:T(8,128)(2,1)S(1)} %get-tuple-element.6, bf16[1,1024,1024]{2,1,0:T(8,128)(2,1)S(1)} %get-tuple-element.5), kind=kLoop, calls=%fused_computation.3 | loop fusion | flops 2097152 | bytes 8388608 | tf_op jit(solution)/shard_map/stack | solution.py:40
  7.2 207.6 %modes.1 = f32[2,4,1,2048,128]{4,3,2,1,0:T(8,128)} custom-call(f32[2,32,32,1024]{3,2,1,0:T(8,128)} %bitcast.11, bf16[2,1024,1024]{2,1,0:T(8,128)(2,1)} %pad_maximum_fusion.hx, bf16[2,256,256]{2,1,0:T(8,128)(2,1)} %constant.28.clone.hy, bf16[2,128,128]{2,1,0:T(8,128)(2,1)} %constant.29.clone.hz, f32[128,128]{1,0:T(8,128)} %broadcast_add_fusion.base, f32[256]{0:T(256)} %sym_y.1), custom_call_target="tpu_custom_call" | custom-call | tf_op jit(solution)/shard_map/modes/pallas_call | solution.py:272
  214.8 8.1 %copy.11 = f32[2,128,4,16,1,128]{5,3,2,1,0,4:T(8,128)} copy(f32[2,128,4,16,1,128]{5,3,1,2,0,4:T(8,128)} %bitcast.9) | data formatting | bytes 16777216 | tf_op jit(solution)/shard_map/transpose | solution.py:303
where the time goes:
time: 226 us; the launch traced here: 223 us
  Pallas kernels  208 us (92%)
  local copies, waits for them, and re-layouts  8.86 us (4%)
  other arithmetic  6.4 us (3%)
    pallas_call x1, Pallas kernels, local(): pl.pallas_call(functools.partial(kernel, lefts, rights, near), name='mode...  208 us
    transpose x1, local copies, waits for them, and re-layouts, local(): jnp.transpose(out, (0, 3, 1, 4, 2, 5))  8.1 us

commit v1 on v0

--- a/solution.py
+++ b/solution.py
@@ -15,6 +15,9 @@
 BAND = 16
 LANES = 128
 SLOTS = 3
+NEAR_LIMIT = 50 * 2**20
+SUB = 2
+LAG = 2
 
 
 def transform_table(count):
@@ -35,6 +38,22 @@
     return (cos_low * plus + sin_low * minus).reshape(count, count)
 
 
+def factors_of(count):
+    inner = 1 << ((count.bit_length() - 1) // 2)
+    outer = count // inner
+    column = np.arange(count)
+
+    def angle(row):
+        return 2.0 * np.pi / count * (row[:, None] * column[None, :] % count)
+
+    low = angle(np.arange(inner))
+    high = angle(np.arange(outer) * inner)
+    scale = count ** (-0.5)
+    low = jnp.asarray(np.stack([np.cos(low), np.sin(low)]), jnp.float32)
+    high = jnp.asarray(np.stack([np.cos(high) + np.sin(high), np.cos(high) - np.sin(high)]) * scale, jnp.float32)
+    return low, high
+
+
 def halves_of(table):
     upper = lax.reduce_precision(table, 8, 7)
     return jnp.stack([upper.astype(jnp.bfloat16), (table - upper).astype(jnp.bfloat16)])
@@ -62,7 +81,7 @@
     pltpu.make_async_copy(ref, ref, sem).wait()
 
 
-def kernel(lefts, rights, near, data, hx, hy, hz, base, sym_y, out, *rest):
+def far_kernel(lefts, rights, near, data, hx, hy, hz, base, sym_y, out, *rest):
     (first, second, dbuf, lines, send_a, send_b, obuf,
      d_sem, sa_sem, ra_sem, y_sem, sb_sem, rb_sem, z_sem, o_sem, *staging) = rest
     fields, share_y, share_z, _ = data.shape
@@ -252,7 +271,376 @@
         put(n).wait()
 
 
-def local(lefts, rights, tracer, symbol_x, symbol_y, symbol_z):
+def stacked(halves):
+    upper, lower = halves[0], halves[1]
+    return jnp.concatenate(
+        [jnp.concatenate([upper, lower], axis=1), jnp.concatenate([upper, jnp.zeros_like(lower)], axis=1)], axis=0
+    )
+
+
+def near_kernel(lefts, rights, data, low_in, high_in, hy_in, hz_in, sym_x, sym_z, sym_y, out, *rest):
+    (first, second, dbuf, low, high, hx, hy, hz, lines, send_a, send_b, base,
+     d_sem, t_sem, sa_sem, ra_sem, sb_sem, rb_sem, sc_sem, rc_sem) = rest
+    fields, share_y, share_z, size_x = data.shape
+    size_y = hy.shape[1]
+    share_x, size_z = base.shape
+    bands = out.shape[1]
+    pieces = share_z // DEPTH
+    chunks = fields * pieces
+    subs = DEPTH // SUB
+    line_subs = pieces * subs
+    out_y = bands * BAND
+    half = rights // 2
+    left, right = lax.axis_index("left"), lax.axis_index("right")
+
+    def load(i):
+        slot = lax.rem(i, 2)
+        planes = pl.ds(lax.rem(i, pieces) * DEPTH, DEPTH)
+        return [pltpu.make_async_copy(
+            data.at[i // pieces, :, planes, pl.ds(c * LANES, LANES)],
+            dbuf.at[slot, c].reshape(share_y, DEPTH, LANES),
+            d_sem.at[slot, c],
+        ) for c in range(size_x // LANES)]
+
+    def fetch(i):
+        for copy in load(i):
+            copy.start()
+
+    tables = [pltpu.make_async_copy(a, b, t_sem.at[n]) for n, (a, b) in enumerate(
+        [(low_in, low), (high_in, high), (hy_in, hy), (hz_in, hz)])]
+    tables[0].start()
+    tables[1].start()
+    fetch(0)
+    tables[2].start()
+    tables[3].start()
+
+    barrier = pltpu.get_barrier_semaphore()
+    for k in range(1, lefts):
+        pl.semaphore_signal(barrier, inc=1, device_id=(lax.rem(left + k, lefts), right), device_id_type=MESH)
+    for k in range(1, rights):
+        pl.semaphore_signal(barrier, inc=1, device_id=(left, lax.rem(right + k, rights)), device_id_type=MESH)
+
+    column = jnp.broadcast_to(sym_x[pl.ds(left, 1), :], (size_z, share_x)).T
+    base[...] = column + sym_z[...]
+
+    pl.semaphore_wait(barrier, lefts + rights - 2)
+
+    def copy_a(i, sub, to):
+        slot = lax.rem(i, SLOTS)
+        return pltpu.make_async_remote_copy(
+            src_ref=send_a.at[slot, to, pl.ds(sub * SUB, SUB)],
+            dst_ref=first.at[i, pl.ds(sub * SUB, SUB), pl.ds(left * share_y, share_y), :],
+            send_sem=sa_sem.at[slot, sub, to],
+            recv_sem=ra_sem.at[i, sub, left],
+            device_id=(to, right),
+            device_id_type=MESH,
+        )
+
+    def copy_b(p, to):
+        field, spot = p // line_subs, lax.rem(p, line_subs) * SUB
+        return pltpu.make_async_remote_copy(
+            src_ref=send_b.at[field, to, :, pl.ds(spot * BAND, SUB * BAND), :],
+            dst_ref=second.at[field, :, pl.ds((right * share_z + spot) * BAND, SUB * BAND), :],
+            send_sem=sb_sem.at[p, to],
+            recv_sem=rb_sem.at[p, right],
+            device_id=(left, to),
+            device_id_type=MESH,
+        )
+
+    def copy_c(band, to):
+        return pltpu.make_async_remote_copy(
+            src_ref=send_b.at[fields - 1, to, band],
+            dst_ref=second.at[fields - 1, band, pl.ds(right * share_z * BAND, share_z * BAND), :],
+            send_sem=sc_sem.at[band, to],
+            recv_sem=rc_sem.at[band, right],
+            device_id=(left, to),
+            device_id_type=MESH,
+        )
+
+    lower = right < half
+    rank = jnp.where(lower, right, rights - 1 - right)
+    end = rank == 0
+
+    def mirrored(t):
+        return jnp.where(lower, t, rights - 1 - t)
+
+    def crossing(k):
+        return mirrored(jnp.where(end, rights - 1 - k, half + k))
+
+    def beside(k):
+        return mirrored(lax.rem(rank + 1 + k, half))
+
+    def sent_a(i):
+        for sub in range(subs):
+            for k in range(1, lefts):
+                copy_a(i, sub, lax.rem(left + k, lefts)).wait_send()
+
+    def widen(cols):
+        for top in range(size_x // low.shape[1]):
+            made = low[0, :, cols] * high[0, top:top + 1, cols] + low[1, :, cols] * high[1, top:top + 1, cols]
+            rows = pl.ds(top * low.shape[1], low.shape[1])
+            hx[0, rows, cols], hx[1, rows, cols] = split(made)
+
+    def x_step(i, opening):
+        slot = lax.rem(i, SLOTS)
+        for copy in load(i):
+            copy.wait()
+
+        if not opening:
+            @pl.when(i >= SLOTS)
+            def _():
+                sent_a(i - SLOTS)
+
+        here = dbuf.at[lax.rem(i, 2)]
+        for c in range(size_x // LANES):
+            cols = pl.ds(c * LANES, LANES)
+            for z in range(DEPTH):
+                rows = pl.ds(z * share_y, share_y)
+                lines[0, rows, cols], lines[1, rows, cols] = split(here[c, pl.ds(z, share_y, stride=DEPTH), :])
+
+        @pl.when(i + 2 < chunks)
+        def _():
+            fetch(i + 2)
+
+        def tile(j, carry):
+            pair = left // 2 ^ (lefts // 2 - 1 - j) if lefts & (lefts - 1) == 0 else j
+            cols = pl.ds(pl.multiple_of(pair * 2 * share_x, 2 * share_x), 2 * share_x)
+            if opening:
+                widen(cols)
+            got = product((lines[0], lines[1]), (hx[0, :, cols], hx[1, :, cols]))
+            for core in range(2):
+                to = 2 * pair + core
+                send_a[slot, to] = got[:, core * share_x:(core + 1) * share_x].reshape(DEPTH, share_y, share_x)
+
+                @pl.when(to != left)
+                def _():
+                    copy_a(i, 0, to).start()
+            return carry
+
+        lax.fori_loop(0, lefts // 2, tile, 0)
+        for sub in range(1, subs):
+            for k in range(lefts - 1, 0, -1):
+                copy_a(i, sub, left ^ k if lefts & (lefts - 1) == 0 else lax.rem(left + k, lefts)).start()
+        first[i, :, pl.ds(pl.multiple_of(left * share_y, share_y), share_y), :] = send_a[slot, left]
+
+    def y_step(i, sub, p):
+        for k in range(1, lefts):
+            who = lax.rem(left + k, lefts)
+            landed(first.at[i, pl.ds(sub * SUB, SUB), pl.ds(who * share_y, share_y), :], ra_sem.at[i, sub, who])
+        field = i // pieces
+        for z in range(0, SUB, 2):
+            pair = jnp.concatenate([first[i, sub * SUB + z], first[i, sub * SUB + z + 1]], axis=1)
+            got = product((hy[0], hy[1]), split(pair))
+            spot = (lax.rem(i, pieces) * DEPTH + sub * SUB + z) * BAND
+            for to in range(rights):
+                for band in range(bands):
+                    top = to * out_y + band * BAND
+                    for side in range(2):
+                        rows = pl.ds(pl.multiple_of(spot + side * BAND, BAND), BAND)
+                        send_b[field, to, band, rows, :] = got[top:top + BAND, side * share_x:(side + 1) * share_x]
+        for k in range(half):
+            @pl.when(jnp.logical_not(end))
+            def _():
+                copy_b(p, crossing(k)).start()
+        for k in range(half - 1):
+            copy_b(p, beside(k)).start()
+        spot = (lax.rem(i, pieces) * DEPTH + sub * SUB) * BAND
+        for band in range(bands):
+            mine = send_b[field, right, band, pl.ds(pl.multiple_of(spot, BAND), SUB * BAND), :]
+            there = pl.multiple_of(right * share_z * BAND + spot, BAND)
+            second[field, band, pl.ds(there, SUB * BAND), :] = mine
+
+    held = (fields - 1) * line_subs
+
+    def late(q):
+        for k in range(half):
+            copy_b(q, crossing(k)).start()
+
+    fetch(1)
+    tables[0].wait()
+    tables[1].wait()
+    x_step(0, True)
+
+    def step(i, carry):
+        @pl.when(i + 1 < chunks)
+        def _():
+            x_step(i + 1, False)
+
+        @pl.when(i == 0)
+        def _():
+            tables[2].wait()
+            tables[3].wait()
+
+        def part(sub, carry):
+            p = i * subs + sub
+            y_step(i, sub, p)
+
+            @pl.when(jnp.logical_and(end, jnp.logical_and(lax.rem(p, LAG) == 0, p // LAG < held)))
+            def _():
+                late(p // LAG)
+
+            return carry
+
+        lax.fori_loop(0, subs, part, 0)
+        return carry
+
+    lax.fori_loop(0, chunks, step, 0)
+
+    @pl.when(end)
+    def _():
+        def more(q, carry):
+            late(q)
+            return carry
+
+        lax.fori_loop(min((chunks * subs + LAG - 1) // LAG, held), held, more, 0)
+        for band in range(bands):
+            for k in range(half):
+                copy_c(band, crossing(k)).start()
+
+    def by_band(who):
+        if who not in (0, rights - 1):
+            return False
+        return right >= half if who < half else right < half
+
+    def arrive(p, carry):
+        for who in range(rights):
+            awaited = right != who
+            if by_band(who) is not False:
+                awaited = jnp.logical_and(awaited, jnp.logical_not(jnp.logical_and(by_band(who), p >= held)))
+
+            @pl.when(awaited)
+            def _():
+                field, spot = p // line_subs, lax.rem(p, line_subs) * SUB
+                ref = second.at[field, :, pl.ds((who * share_z + spot) * BAND, SUB * BAND), :]
+                landed(ref, rb_sem.at[p, who])
+        return carry
+
+    def z_step(n, carry):
+        field, band = n // bands, lax.rem(n, bands)
+
+        @pl.when(band == 0)
+        def _():
+            lax.fori_loop(field * line_subs, (field + 1) * line_subs, arrive, 0)
+
+        @pl.when(field == fields - 1)
+        def _():
+            for who in (0, rights - 1):
+                @pl.when(by_band(who))
+                def _():
+                    ref = second.at[field, band, pl.ds(who * share_z * BAND, share_z * BAND), :]
+                    landed(ref, rc_sem.at[band, who])
+
+        table = hz[...]
+
+        def line(y, carry):
+            plane = second[field, band, pl.ds(y, size_z, stride=BAND), :].T
+            got = jnp.dot(jnp.concatenate(split(plane), axis=1), table, preferred_element_type=jnp.float32)
+            got = (got[:, :size_z] + got[:, size_z:]) * lax.rsqrt(base[...] + sym_y[right * out_y + band * BAND + y])
+            out[field, band, pl.ds(y, share_x, stride=BAND), :] = got
+            return carry
+
+        lax.fori_loop(0, BAND, line, 0, unroll=4)
+        return carry
+
+    lax.fori_loop(0, fields * bands, z_step, 0)
+
+    def drain_a(i, carry):
+        sent_a(i)
+        return carry
+
+    lax.fori_loop(max(chunks - SLOTS, 0), chunks, drain_a, 0)
+
+    def drain_b(p, carry):
+        for k in range(half - 1):
+            copy_b(p, beside(k)).wait_send()
+
+        @pl.when(jnp.logical_or(jnp.logical_not(end), p < held))
+        def _():
+            for k in range(half):
+                copy_b(p, crossing(k)).wait_send()
+
+        return carry
+
+    lax.fori_loop(0, chunks * subs, drain_b, 0)
+
+    @pl.when(end)
+    def _():
+        for band in range(bands):
+            for k in range(half):
+                copy_c(band, crossing(k)).wait_send()
+
+
+def flush_kernel(ready, out, sem):
+    fields, bands = ready.shape[:2]
+    copies = []
+    for n in range(fields * bands):
+        field, band = n // bands, n % bands
+        there = out.at[field, :, pl.ds(band * BAND, BAND), :]
+        copies.append(pltpu.make_async_copy(ready.at[field, band], there, sem.at[n]))
+    for copy in copies:
+        copy.start()
+    for copy in copies:
+        copy.wait()
+
+
+def near_local(lefts, rights, tracer, symbol_x, symbol_y, symbol_z):
+    fields, size_x, share_y, share_z = tracer.shape
+    size_y, size_z = symbol_y.shape[0], symbol_z.shape[0]
+    share_x, out_y = size_x // lefts, size_y // rights
+    bands = out_y // BAND
+    chunks = fields * (share_z // DEPTH)
+    parts = chunks * (DEPTH // SUB)
+    data = jnp.transpose(tracer, (0, 2, 3, 1))
+    low, high = factors_of(size_x)
+    hy, hz = small_table(size_y), stacked(small_table(size_z))
+    f32, bf16 = jnp.float32, jnp.bfloat16
+    any_space = pl.BlockSpec(memory_space=pl.ANY)
+    vmem = pl.BlockSpec(memory_space=pltpu.VMEM)
+    dma = pltpu.SemaphoreType.DMA
+    ready = pl.pallas_call(
+        functools.partial(near_kernel, lefts, rights),
+        name="modes",
+        out_shape=pltpu.VMEM((fields, bands, share_x * BAND, size_z), f32),
+        in_specs=[*[any_space] * 5, vmem, vmem, pl.BlockSpec(memory_space=pltpu.SMEM)],
+        out_specs=vmem,
+        scratch_shapes=[
+            pltpu.VMEM((chunks, DEPTH, size_y, share_x), f32),
+            pltpu.VMEM((fields, bands, size_z * BAND, share_x), f32),
+            pltpu.VMEM((2, size_x // LANES, share_y * DEPTH, LANES), f32),
+            pltpu.VMEM(low.shape, f32),
+            pltpu.VMEM(high.shape, f32),
+            pltpu.VMEM((2, size_x, size_x), bf16),
+            pltpu.VMEM(hy.shape, bf16),
+            pltpu.VMEM(hz.shape, bf16),
+            pltpu.VMEM((2, share_y * DEPTH, size_x), bf16),
+            pltpu.VMEM((SLOTS, lefts, DEPTH, share_y, share_x), f32),
+            pltpu.VMEM((fields, rights, bands, share_z * BAND, share_x), f32),
+            pltpu.VMEM((share_x, size_z), f32),
+            dma((2, size_x // LANES)),
+            dma((4,)),
+            dma((SLOTS, DEPTH // SUB, lefts)),
+            dma((chunks, DEPTH // SUB, lefts)),
+            dma((parts, rights)),
+            dma((parts, rights)),
+            dma((bands, rights)),
+            dma((bands, rights)),
+        ],
+        compiler_params=pltpu.CompilerParams(
+            collective_id=0, has_side_effects=True, vmem_limit_bytes=NEAR_LIMIT
+        ),
+    )(data, low, high, hy, hz, symbol_x.reshape(lefts, share_x), symbol_z.reshape(1, size_z), symbol_y)
+    return pl.pallas_call(
+        flush_kernel,
+        name="flush",
+        out_shape=jax.ShapeDtypeStruct((fields, share_x, out_y, size_z), f32),
+        in_specs=[vmem],
+        out_specs=any_space,
+        scratch_shapes=[dma((fields * bands,))],
+        compiler_params=pltpu.CompilerParams(vmem_limit_bytes=2**21),
+    )(ready.reshape(fields, bands, share_x, BAND, size_z))
+
+
+def far_local(lefts, rights, tracer, symbol_x, symbol_y, symbol_z):
     fields, size_x, share_y, share_z = tracer.shape
     size_y, size_z = symbol_y.shape[0], symbol_z.shape[0]
     share_x, out_y = size_x // lefts, size_y // rights
@@ -270,7 +658,7 @@
         pltpu.VMEM((size_y * DEPTH, share_x), f32), pltpu.VMEM((size_z * BAND, share_x), f32)
     ]
     results = pl.pallas_call(
-        functools.partial(kernel, lefts, rights, near),
+        functools.partial(far_kernel, lefts, rights, near),
         name="modes",
         out_shape=[
             jax.ShapeDtypeStruct((fields, bands, size_z // LANES, share_x * BAND, LANES), f32),
@@ -303,6 +691,15 @@
     return jnp.transpose(out, (0, 3, 1, 4, 2, 5)).reshape(fields, share_x, out_y, size_z)
 
 
+def local(lefts, rights, tracer, symbol_x, symbol_y, symbol_z):
+    fields, size_x, share_y, share_z = tracer.shape
+    size_z, share_x = symbol_z.shape[0], size_x // lefts
+    size = 4 * math.prod(tracer.shape)
+    fits = size <= NEAR_BYTES // 2 and share_x == LANES and size_z == LANES and rights % 2 == 0
+    run = near_local if fits else far_local
+    return run(lefts, rights, tracer, symbol_x, symbol_y, symbol_z)
+
+
 def solution(mesh):
     return jax.shard_map(
         functools.partial(local, mesh.shape["left"], mesh.shape["right"]),

time: 226 us -> 210 us (0.929); the launches traced: 223 us -> 210 us
  local copies, waits for them, and re-layouts: 8.86 us -> 0 us
  other arithmetic: 6.4 us -> 0 us
    transpose x1 -> x0, local copies, waits for them, and re-layouts: 8.1 us -> none  [local(): jnp.transpose(out, (0, 3, 1, 4, 2, 5))]
    add x2 -> x0, other arithmetic: 3.08 us -> none  [the longest x1 1.71 us: transform_table(): return (cos_low * plus + sin_low * minus).reshape(count, count)]
    pallas_call x1 -> x2, Pallas kernels: 208 us -> 210 us  [the longest x1 207 us: near_local(): pl.pallas_call(functools.partial(near_kernel, lefts, rights), name='modes...]
    another operation x1 -> x0, other arithmetic: 2.38 us -> none  [halves_of(): jnp.stack([upper.astype(jnp.bfloat16), (table - upper).astype(jnp.bfloat1...]
where the time goes in v1:
time: 210 us
  Pallas kernels  210 us (100%)
    pallas_call x1, Pallas kernels, near_local(): pl.pallas_call(functools.partial(near_kernel, lefts, rights), name='modes...  207 us

profile of v1, /device:TPU:0, one launch (start us, length us, event | category | flops | bytes accessed | tf_op | source)
XLA Modules:
  0.0 210.1 jit_solution(1138529827689295528)
XLA Ops:
  0.0 206.7 %modes.1 = f32[2,4,2048,128]{3,2,1,0:T(8,128)S(1)} custom-call(f32[2,32,32,1024]{3,2,1,0:T(8,128)} %bitcast.5, f32[2,32,1024]{2,1,0:T(8,128)} %constant.10.clone.low_in, f32[2,32,1024]{2,1,0:T(8,128)} %constant.11.clone.high_in, bf16[2,256,256]{2,1,0:T(8,128)(2,1)} %constant.12.clone.hy_in, bf16[256,256]{1,0:T(8,128)(2,1)} %constant.22.hz_in, ...), custom_call_target="tpu_custom_call" | custom-call | tf_op jit(solution)/shard_map/modes/pallas_call | solution.py:600
  206.7 3.4 %flush.1 = f32[2,128,64,128]{3,2,1,0:T(8,128)} custom-call(f32[2,4,128,16,128]{4,3,2,1,0:T(8,128)S(1)} %bitcast.4), custom_call_target="tpu_custom_call" | custom-call | tf_op jit(solution)/shard_map/flush/pallas_call | solution.py:632

commit v2 on v1

--- a/solution.py
+++ b/solution.py
@@ -17,7 +17,6 @@
 SLOTS = 3
 NEAR_LIMIT = 50 * 2**20
 SUB = 2
-LAG = 2
 
 
 def transform_table(count):
@@ -280,7 +279,7 @@
 
 def near_kernel(lefts, rights, data, low_in, high_in, hy_in, hz_in, sym_x, sym_z, sym_y, out, *rest):
     (first, second, dbuf, low, high, hx, hy, hz, lines, send_a, send_b, base,
-     d_sem, t_sem, sa_sem, ra_sem, sb_sem, rb_sem, sc_sem, rc_sem) = rest
+     d_sem, t_sem, sa_sem, ra_sem, sb_sem, rb_sem, rc_sem) = rest
     fields, share_y, share_z, size_x = data.shape
     size_y = hy.shape[1]
     share_x, size_z = base.shape
@@ -299,7 +298,7 @@
         return [pltpu.make_async_copy(
             data.at[i // pieces, :, planes, pl.ds(c * LANES, LANES)],
             dbuf.at[slot, c].reshape(share_y, DEPTH, LANES),
-            d_sem.at[slot, c],
+            d_sem.at[slot],
         ) for c in range(size_x // LANES)]
 
     def fetch(i):
@@ -323,15 +322,12 @@
     column = jnp.broadcast_to(sym_x[pl.ds(left, 1), :], (size_z, share_x)).T
     base[...] = column + sym_z[...]
 
-    pl.semaphore_wait(barrier, lefts + rights - 2)
-
     def copy_a(i, sub, to):
-        slot = lax.rem(i, SLOTS)
         return pltpu.make_async_remote_copy(
-            src_ref=send_a.at[slot, to, pl.ds(sub * SUB, SUB)],
+            src_ref=send_a.at[i, to, pl.ds(sub * SUB, SUB)],
             dst_ref=first.at[i, pl.ds(sub * SUB, SUB), pl.ds(left * share_y, share_y), :],
-            send_sem=sa_sem.at[slot, sub, to],
-            recv_sem=ra_sem.at[i, sub, left],
+            send_sem=sa_sem,
+            recv_sem=ra_sem.at[i, sub],
             device_id=(to, right),
             device_id_type=MESH,
         )
@@ -341,8 +337,8 @@
         return pltpu.make_async_remote_copy(
             src_ref=send_b.at[field, to, :, pl.ds(spot * BAND, SUB * BAND), :],
             dst_ref=second.at[field, :, pl.ds((right * share_z + spot) * BAND, SUB * BAND), :],
-            send_sem=sb_sem.at[p, to],
-            recv_sem=rb_sem.at[p, right],
+            send_sem=sb_sem,
+            recv_sem=rb_sem.at[field],
             device_id=(left, to),
             device_id_type=MESH,
         )
@@ -351,12 +347,13 @@
         return pltpu.make_async_remote_copy(
             src_ref=send_b.at[fields - 1, to, band],
             dst_ref=second.at[fields - 1, band, pl.ds(right * share_z * BAND, share_z * BAND), :],
-            send_sem=sc_sem.at[band, to],
-            recv_sem=rc_sem.at[band, right],
+            send_sem=sb_sem,
+            recv_sem=rc_sem.at[band],
             device_id=(left, to),
             device_id_type=MESH,
         )
 
+    held = (fields - 1) * line_subs
     lower = right < half
     rank = jnp.where(lower, right, rights - 1 - right)
     end = rank == 0
@@ -369,11 +366,6 @@
 
     def beside(k):
         return mirrored(lax.rem(rank + 1 + k, half))
-
-    def sent_a(i):
-        for sub in range(subs):
-            for k in range(1, lefts):
-                copy_a(i, sub, lax.rem(left + k, lefts)).wait_send()
 
     def widen(cols):
         for top in range(size_x // low.shape[1]):
@@ -381,52 +373,55 @@
             rows = pl.ds(top * low.shape[1], low.shape[1])
             hx[0, rows, cols], hx[1, rows, cols] = split(made)
 
+    def partner(k):
+        return left ^ k if lefts & (lefts - 1) == 0 else lax.rem(left + k, lefts)
+
+    def x_tile(i, j, opening):
+        pair = partner(lefts - 1 - 2 * j) // 2
+        cols = pl.ds(pl.multiple_of(pair * 2 * share_x, 2 * share_x), 2 * share_x)
+        if opening:
+            widen(cols)
+        got = product((lines[0], lines[1]), (hx[0, :, cols], hx[1, :, cols]))
+        for core in range(2):
+            send_a[i, 2 * pair + core] = got[:, core * share_x:(core + 1) * share_x].reshape(DEPTH, share_y, share_x)
+        return pair
+
+    def x_send(i, pair):
+        for core in range(2):
+            @pl.when(2 * pair + core != left)
+            def _():
+                copy_a(i, 0, 2 * pair + core).start()
+
     def x_step(i, opening):
-        slot = lax.rem(i, SLOTS)
-        for copy in load(i):
-            copy.wait()
-
-        if not opening:
-            @pl.when(i >= SLOTS)
-            def _():
-                sent_a(i - SLOTS)
-
-        here = dbuf.at[lax.rem(i, 2)]
+        slot = lax.rem(i, 2)
+        landed(dbuf.at[slot], d_sem.at[slot])
         for c in range(size_x // LANES):
             cols = pl.ds(c * LANES, LANES)
             for z in range(DEPTH):
                 rows = pl.ds(z * share_y, share_y)
-                lines[0, rows, cols], lines[1, rows, cols] = split(here[c, pl.ds(z, share_y, stride=DEPTH), :])
+                lines[0, rows, cols], lines[1, rows, cols] = split(dbuf[slot, c, pl.ds(z, share_y, stride=DEPTH), :])
 
         @pl.when(i + 2 < chunks)
         def _():
             fetch(i + 2)
 
+        if opening:
+            pair = x_tile(i, 0, True)
+            pl.semaphore_wait(barrier, lefts + rights - 2)
+            x_send(i, pair)
+
         def tile(j, carry):
-            pair = left // 2 ^ (lefts // 2 - 1 - j) if lefts & (lefts - 1) == 0 else j
-            cols = pl.ds(pl.multiple_of(pair * 2 * share_x, 2 * share_x), 2 * share_x)
-            if opening:
-                widen(cols)
-            got = product((lines[0], lines[1]), (hx[0, :, cols], hx[1, :, cols]))
-            for core in range(2):
-                to = 2 * pair + core
-                send_a[slot, to] = got[:, core * share_x:(core + 1) * share_x].reshape(DEPTH, share_y, share_x)
-
-                @pl.when(to != left)
-                def _():
-                    copy_a(i, 0, to).start()
+            x_send(i, x_tile(i, j, opening))
             return carry
 
-        lax.fori_loop(0, lefts // 2, tile, 0)
+        lax.fori_loop(1 if opening else 0, lefts // 2, tile, 0)
         for sub in range(1, subs):
             for k in range(lefts - 1, 0, -1):
-                copy_a(i, sub, left ^ k if lefts & (lefts - 1) == 0 else lax.rem(left + k, lefts)).start()
-        first[i, :, pl.ds(pl.multiple_of(left * share_y, share_y), share_y), :] = send_a[slot, left]
+                copy_a(i, sub, partner(k)).start()
+        first[i, :, pl.ds(pl.multiple_of(left * share_y, share_y), share_y), :] = send_a[i, left]
 
     def y_step(i, sub, p):
-        for k in range(1, lefts):
-            who = lax.rem(left + k, lefts)
-            landed(first.at[i, pl.ds(sub * SUB, SUB), pl.ds(who * share_y, share_y), :], ra_sem.at[i, sub, who])
+        landed(first.at[i, pl.ds(sub * SUB, SUB), pl.ds(0, (lefts - 1) * share_y), :], ra_sem.at[i, sub])
         field = i // pieces
         for z in range(0, SUB, 2):
             pair = jnp.concatenate([first[i, sub * SUB + z], first[i, sub * SUB + z + 1]], axis=1)
@@ -439,7 +434,7 @@
                         rows = pl.ds(pl.multiple_of(spot + side * BAND, BAND), BAND)
                         send_b[field, to, band, rows, :] = got[top:top + BAND, side * share_x:(side + 1) * share_x]
         for k in range(half):
-            @pl.when(jnp.logical_not(end))
+            @pl.when(jnp.logical_or(end, p < held))
             def _():
                 copy_b(p, crossing(k)).start()
         for k in range(half - 1):
@@ -450,85 +445,46 @@
             there = pl.multiple_of(right * share_z * BAND + spot, BAND)
             second[field, band, pl.ds(there, SUB * BAND), :] = mine
 
-    held = (fields - 1) * line_subs
-
-    def late(q):
-        for k in range(half):
-            copy_b(q, crossing(k)).start()
-
     fetch(1)
     tables[0].wait()
     tables[1].wait()
     x_step(0, True)
+    tables[2].wait()
+    tables[3].wait()
 
     def step(i, carry):
+        y_step(i, 0, i * subs)
+
         @pl.when(i + 1 < chunks)
         def _():
             x_step(i + 1, False)
 
-        @pl.when(i == 0)
-        def _():
-            tables[2].wait()
-            tables[3].wait()
-
         def part(sub, carry):
-            p = i * subs + sub
-            y_step(i, sub, p)
-
-            @pl.when(jnp.logical_and(end, jnp.logical_and(lax.rem(p, LAG) == 0, p // LAG < held)))
-            def _():
-                late(p // LAG)
-
+            y_step(i, sub, i * subs + sub)
             return carry
 
-        lax.fori_loop(0, subs, part, 0)
+        lax.fori_loop(1, subs, part, 0)
         return carry
 
     lax.fori_loop(0, chunks, step, 0)
 
-    @pl.when(end)
+    @pl.when(jnp.logical_not(end))
     def _():
-        def more(q, carry):
-            late(q)
-            return carry
-
-        lax.fori_loop(min((chunks * subs + LAG - 1) // LAG, held), held, more, 0)
         for band in range(bands):
             for k in range(half):
                 copy_c(band, crossing(k)).start()
 
-    def by_band(who):
-        if who not in (0, rights - 1):
-            return False
-        return right >= half if who < half else right < half
-
-    def arrive(p, carry):
-        for who in range(rights):
-            awaited = right != who
-            if by_band(who) is not False:
-                awaited = jnp.logical_and(awaited, jnp.logical_not(jnp.logical_and(by_band(who), p >= held)))
-
-            @pl.when(awaited)
-            def _():
-                field, spot = p // line_subs, lax.rem(p, line_subs) * SUB
-                ref = second.at[field, :, pl.ds((who * share_z + spot) * BAND, SUB * BAND), :]
-                landed(ref, rb_sem.at[p, who])
-        return carry
-
     def z_step(n, carry):
         field, band = n // bands, lax.rem(n, bands)
 
-        @pl.when(band == 0)
-        def _():
-            lax.fori_loop(field * line_subs, (field + 1) * line_subs, arrive, 0)
+        for sources, chosen in ((rights - 1, field < fields - 1), (half, field == fields - 1)):
+            @pl.when(jnp.logical_and(band == 0, chosen))
+            def _():
+                landed(second.at[field, :, pl.ds(0, sources * share_z * BAND), :], rb_sem.at[field])
 
         @pl.when(field == fields - 1)
         def _():
-            for who in (0, rights - 1):
-                @pl.when(by_band(who))
-                def _():
-                    ref = second.at[field, band, pl.ds(who * share_z * BAND, share_z * BAND), :]
-                    landed(ref, rc_sem.at[band, who])
+            landed(second.at[field, band, pl.ds(0, (half - 1) * share_z * BAND), :], rc_sem.at[band])
 
         table = hz[...]
 
@@ -544,43 +500,17 @@
 
     lax.fori_loop(0, fields * bands, z_step, 0)
 
-    def drain_a(i, carry):
-        sent_a(i)
-        return carry
-
-    lax.fori_loop(max(chunks - SLOTS, 0), chunks, drain_a, 0)
-
-    def drain_b(p, carry):
-        for k in range(half - 1):
-            copy_b(p, beside(k)).wait_send()
-
-        @pl.when(jnp.logical_or(jnp.logical_not(end), p < held))
-        def _():
-            for k in range(half):
-                copy_b(p, crossing(k)).wait_send()
-
-        return carry
-
-    lax.fori_loop(0, chunks * subs, drain_b, 0)
-
-    @pl.when(end)
-    def _():
-        for band in range(bands):
-            for k in range(half):
-                copy_c(band, crossing(k)).wait_send()
+    landed(send_a.at[:, pl.ds(0, lefts - 1)], sa_sem)
+    landed(send_b.at[:, pl.ds(0, rights - 1)], sb_sem)
 
 
 def flush_kernel(ready, out, sem):
     fields, bands = ready.shape[:2]
-    copies = []
     for n in range(fields * bands):
         field, band = n // bands, n % bands
         there = out.at[field, :, pl.ds(band * BAND, BAND), :]
-        copies.append(pltpu.make_async_copy(ready.at[field, band], there, sem.at[n]))
-    for copy in copies:
-        copy.start()
-    for copy in copies:
-        copy.wait()
+        pltpu.make_async_copy(ready.at[field, band], there, sem).start()
+    landed(out, sem)
 
 
 def near_local(lefts, rights, tracer, symbol_x, symbol_y, symbol_z):
@@ -613,17 +543,16 @@
             pltpu.VMEM(hy.shape, bf16),
             pltpu.VMEM(hz.shape, bf16),
             pltpu.VMEM((2, share_y * DEPTH, size_x), bf16),
-            pltpu.VMEM((SLOTS, lefts, DEPTH, share_y, share_x), f32),
+            pltpu.VMEM((chunks, lefts, DEPTH, share_y, share_x), f32),
             pltpu.VMEM((fields, rights, bands, share_z * BAND, share_x), f32),
             pltpu.VMEM((share_x, size_z), f32),
-            dma((2, size_x // LANES)),
+            dma((2,)),
             dma((4,)),
-            dma((SLOTS, DEPTH // SUB, lefts)),
-            dma((chunks, DEPTH // SUB, lefts)),
-            dma((parts, rights)),
-            dma((parts, rights)),
-            dma((bands, rights)),
-            dma((bands, rights)),
+            dma,
+            dma((chunks, DEPTH // SUB)),
+            dma,
+            dma((fields,)),
+            dma((bands,)),
         ],
         compiler_params=pltpu.CompilerParams(
             collective_id=0, has_side_effects=True, vmem_limit_bytes=NEAR_LIMIT
@@ -635,7 +564,7 @@
         out_shape=jax.ShapeDtypeStruct((fields, share_x, out_y, size_z), f32),
         in_specs=[vmem],
         out_specs=any_space,
-        scratch_shapes=[dma((fields * bands,))],
+        scratch_shapes=[dma],
         compiler_params=pltpu.CompilerParams(vmem_limit_bytes=2**21),
     )(ready.reshape(fields, bands, share_x, BAND, size_z))
 

time: 210 us -> 199 us (0.948)
  Pallas kernels: 210 us -> 198 us
    pallas_call x1, Pallas kernels: 207 us -> 195 us  [near_local(): pl.pallas_call(functools.partial(near_kernel, lefts, rights), name='modes...]
where the time goes in v2:
time: 199 us; the launch traced here: 198 us
  Pallas kernels  198 us (99%)
    pallas_call x1, Pallas kernels, near_local(): pl.pallas_call(functools.partial(near_kernel, lefts, rights), name='modes...  195 us

profile of v2, /device:TPU:0, one launch (start us, length us, event | category | flops | bytes accessed | tf_op | source)
XLA Modules:
  0.0 198.4 jit_solution(939751661544521364)
XLA Ops:
  0.0 195.1 %modes.1 = f32[2,4,2048,128]{3,2,1,0:T(8,128)S(1)} custom-call(f32[2,32,32,1024]{3,2,1,0:T(8,128)} %bitcast.5, f32[2,32,1024]{2,1,0:T(8,128)} %constant.10.clone.low_in, f32[2,32,1024]{2,1,0:T(8,128)} %constant.11.clone.high_in, bf16[2,256,256]{2,1,0:T(8,128)(2,1)} %constant.12.clone.hy_in, bf16[256,256]{1,0:T(8,128)(2,1)} %constant.22.hz_in, ...), custom_call_target="tpu_custom_call" | custom-call | tf_op jit(solution)/shard_map/modes/pallas_call | solution.py:530
  195.1 3.3 %flush.1 = f32[2,128,64,128]{3,2,1,0:T(8,128)} custom-call(f32[2,4,128,16,128]{4,3,2,1,0:T(8,128)S(1)} %bitcast.4), custom_call_target="tpu_custom_call" | custom-call | tf_op jit(solution)/shard_map/flush/pallas_call | solution.py:561

commit v3 on v2

--- a/solution.py
+++ b/solution.py
@@ -13,6 +13,7 @@
 NEAR_BYTES = 20 * 2**20
 DEPTH = 8
 BAND = 16
+SUBLANES = 8
 LANES = 128
 SLOTS = 3
 NEAR_LIMIT = 50 * 2**20
@@ -277,9 +278,9 @@
     )
 
 
-def near_kernel(lefts, rights, data, low_in, high_in, hy_in, hz_in, sym_x, sym_z, sym_y, out, *rest):
+def near_kernel(lefts, rights, data, low_in, high_in, hy_in, hz_in, x_in, z_in, y_in, out, *rest):
     (first, second, dbuf, low, high, hx, hy, hz, lines, send_a, send_b, base,
-     d_sem, t_sem, sa_sem, ra_sem, sb_sem, rb_sem, rc_sem) = rest
+     sym_x, sym_z, sym_y, d_sem, t_sem, sa_sem, ra_sem, rp_sem, sb_sem, rb_sem, rc_sem) = rest
     fields, share_y, share_z, size_x = data.shape
     size_y = hy.shape[1]
     share_x, size_z = base.shape
@@ -287,7 +288,6 @@
     pieces = share_z // DEPTH
     chunks = fields * pieces
     subs = DEPTH // SUB
-    line_subs = pieces * subs
     out_y = bands * BAND
     half = rights // 2
     left, right = lax.axis_index("left"), lax.axis_index("right")
@@ -306,12 +306,12 @@
             copy.start()
 
     tables = [pltpu.make_async_copy(a, b, t_sem.at[n]) for n, (a, b) in enumerate(
-        [(low_in, low), (high_in, high), (hy_in, hy), (hz_in, hz)])]
+        [(low_in, low), (high_in, high), (hy_in, hy), (hz_in, hz), (x_in, sym_x), (z_in, sym_z), (y_in, sym_y)])]
     tables[0].start()
     tables[1].start()
     fetch(0)
-    tables[2].start()
-    tables[3].start()
+    for table in tables[2:]:
+        table.start()
 
     barrier = pltpu.get_barrier_semaphore()
     for k in range(1, lefts):
@@ -319,41 +319,38 @@
     for k in range(1, rights):
         pl.semaphore_signal(barrier, inc=1, device_id=(left, lax.rem(right + k, rights)), device_id_type=MESH)
 
-    column = jnp.broadcast_to(sym_x[pl.ds(left, 1), :], (size_z, share_x)).T
-    base[...] = column + sym_z[...]
-
-    def copy_a(i, sub, to):
+    def copy_a(i, z, count, to, sem):
         return pltpu.make_async_remote_copy(
-            src_ref=send_a.at[i, to, pl.ds(sub * SUB, SUB)],
-            dst_ref=first.at[i, pl.ds(sub * SUB, SUB), pl.ds(left * share_y, share_y), :],
+            src_ref=send_a.at[i, to, pl.ds(z, count)],
+            dst_ref=first.at[i, pl.ds(z, count), pl.ds(left * share_y, share_y), :],
             send_sem=sa_sem,
-            recv_sem=ra_sem.at[i, sub],
+            recv_sem=sem,
             device_id=(to, right),
             device_id_type=MESH,
         )
 
-    def copy_b(p, to):
-        field, spot = p // line_subs, lax.rem(p, line_subs) * SUB
+    def copy_b(field, spot, count, to):
         return pltpu.make_async_remote_copy(
-            src_ref=send_b.at[field, to, :, pl.ds(spot * BAND, SUB * BAND), :],
-            dst_ref=second.at[field, :, pl.ds((right * share_z + spot) * BAND, SUB * BAND), :],
+            src_ref=send_b.at[field, to, :, pl.ds(spot * BAND, count * BAND), :],
+            dst_ref=second.at[field, :, pl.ds((right * share_z + spot) * BAND, count * BAND), :],
             send_sem=sb_sem,
             recv_sem=rb_sem.at[field],
             device_id=(left, to),
             device_id_type=MESH,
         )
 
-    def copy_c(band, to):
+    def copy_c(n, to):
+        band, rows = n // 2, pl.ds(n % 2 * SUBLANES, SUBLANES)
+        there = second.at[fields - 1, band].reshape(size_z, BAND, share_x)
         return pltpu.make_async_remote_copy(
-            src_ref=send_b.at[fields - 1, to, band],
-            dst_ref=second.at[fields - 1, band, pl.ds(right * share_z * BAND, share_z * BAND), :],
+            src_ref=send_b.at[fields - 1, to, band].reshape(share_z, BAND, share_x).at[:, rows, :],
+            dst_ref=there.at[pl.ds(right * share_z, share_z), rows, :],
             send_sem=sb_sem,
-            recv_sem=rc_sem.at[band],
+            recv_sem=rc_sem.at[n],
             device_id=(left, to),
             device_id_type=MESH,
         )
 
-    held = (fields - 1) * line_subs
     lower = right < half
     rank = jnp.where(lower, right, rights - 1 - right)
     end = rank == 0
@@ -376,130 +373,173 @@
     def partner(k):
         return left ^ k if lefts & (lefts - 1) == 0 else lax.rem(left + k, lefts)
 
-    def x_tile(i, j, opening):
+    def x_tile(i, j, z, count, opening):
         pair = partner(lefts - 1 - 2 * j) // 2
         cols = pl.ds(pl.multiple_of(pair * 2 * share_x, 2 * share_x), 2 * share_x)
         if opening:
             widen(cols)
-        got = product((lines[0], lines[1]), (hx[0, :, cols], hx[1, :, cols]))
+        rows = pl.ds(z * share_y, count * share_y)
+        got = product((lines[0, rows, :], lines[1, rows, :]), (hx[0, :, cols], hx[1, :, cols]))
         for core in range(2):
-            send_a[i, 2 * pair + core] = got[:, core * share_x:(core + 1) * share_x].reshape(DEPTH, share_y, share_x)
+            part = got[:, core * share_x:(core + 1) * share_x].reshape(count, share_y, share_x)
+            send_a[i, 2 * pair + core, z:z + count] = part
         return pair
 
-    def x_send(i, pair):
+    def x_split(i, planes):
+        slot = lax.rem(i, 2)
+        for c in range(size_x // LANES):
+            cols = pl.ds(c * LANES, LANES)
+            for z in planes:
+                rows = pl.ds(z * share_y, share_y)
+                lines[0, rows, cols], lines[1, rows, cols] = split(dbuf[slot, c, pl.ds(z, share_y, stride=DEPTH), :])
+
+    def x_send(i, z, count, pair, sem):
         for core in range(2):
             @pl.when(2 * pair + core != left)
             def _():
-                copy_a(i, 0, 2 * pair + core).start()
-
-    def x_step(i, opening):
+                copy_a(i, z, count, 2 * pair + core, sem).start()
+
+    def x_rest(i, subs_left):
+        for sub in subs_left:
+            for k in range(lefts - 1, 0, -1):
+                copy_a(i, sub * SUB, SUB, partner(k), ra_sem.at[i, sub]).start()
+
+    def x_own(i, z, count):
+        mine = pl.ds(pl.multiple_of(left * share_y, share_y), share_y)
+        first[i, z:z + count, mine, :] = send_a[i, left, z:z + count]
+
+    def x_open():
+        landed(dbuf.at[0], d_sem.at[0])
+        x_split(0, range(SUB))
+        pair = x_tile(0, 0, 0, SUB, True)
+        pl.semaphore_wait(barrier, lefts + rights - 2)
+        x_send(0, 0, 1, pair, rp_sem.at[0])
+
+        def tile(j, carry):
+            x_send(0, 0, 1, x_tile(0, j, 0, SUB, True), rp_sem.at[0])
+            return carry
+
+        lax.fori_loop(1, lefts // 2, tile, 0)
+        for z in range(1, SUB):
+            for k in range(lefts - 1, 0, -1):
+                copy_a(0, z, 1, partner(k), rp_sem.at[z]).start()
+        x_own(0, 0, SUB)
+        x_split(0, range(SUB, DEPTH))
+
+        def more(j, carry):
+            x_send(0, SUB, SUB, x_tile(0, j, SUB, DEPTH - SUB, False), ra_sem.at[0, 1])
+            return carry
+
+        lax.fori_loop(0, lefts // 2, more, 0)
+        x_rest(0, range(2, subs))
+        x_own(0, SUB, DEPTH - SUB)
+        fetch(2)
+
+    def x_step(i):
         slot = lax.rem(i, 2)
         landed(dbuf.at[slot], d_sem.at[slot])
-        for c in range(size_x // LANES):
-            cols = pl.ds(c * LANES, LANES)
-            for z in range(DEPTH):
-                rows = pl.ds(z * share_y, share_y)
-                lines[0, rows, cols], lines[1, rows, cols] = split(dbuf[slot, c, pl.ds(z, share_y, stride=DEPTH), :])
+        x_split(i, range(DEPTH))
 
         @pl.when(i + 2 < chunks)
         def _():
             fetch(i + 2)
 
-        if opening:
-            pair = x_tile(i, 0, True)
-            pl.semaphore_wait(barrier, lefts + rights - 2)
-            x_send(i, pair)
-
         def tile(j, carry):
-            x_send(i, x_tile(i, j, opening))
-            return carry
-
-        lax.fori_loop(1 if opening else 0, lefts // 2, tile, 0)
-        for sub in range(1, subs):
-            for k in range(lefts - 1, 0, -1):
-                copy_a(i, sub, partner(k)).start()
-        first[i, :, pl.ds(pl.multiple_of(left * share_y, share_y), share_y), :] = send_a[i, left]
-
-    def y_step(i, sub, p):
-        landed(first.at[i, pl.ds(sub * SUB, SUB), pl.ds(0, (lefts - 1) * share_y), :], ra_sem.at[i, sub])
-        field = i // pieces
-        for z in range(0, SUB, 2):
-            pair = jnp.concatenate([first[i, sub * SUB + z], first[i, sub * SUB + z + 1]], axis=1)
-            got = product((hy[0], hy[1]), split(pair))
-            spot = (lax.rem(i, pieces) * DEPTH + sub * SUB + z) * BAND
-            for to in range(rights):
-                for band in range(bands):
-                    top = to * out_y + band * BAND
-                    for side in range(2):
-                        rows = pl.ds(pl.multiple_of(spot + side * BAND, BAND), BAND)
-                        send_b[field, to, band, rows, :] = got[top:top + BAND, side * share_x:(side + 1) * share_x]
+            x_send(i, 0, SUB, x_tile(i, j, 0, DEPTH, False), ra_sem.at[i, 0])
+            return carry
+
+        lax.fori_loop(0, lefts // 2, tile, 0)
+        x_rest(i, range(1, subs))
+        x_own(i, 0, DEPTH)
+
+    def y_step(i, z, count, sem):
+        landed(first.at[i, pl.ds(z, count), pl.ds(0, (lefts - 1) * share_y), :], sem)
+        field, spot = i // pieces, lax.rem(i, pieces) * DEPTH + z
+        wide = jnp.concatenate([first[i, z + n] for n in range(count)], axis=1)
+        got = product((hy[0], hy[1]), split(wide))
+        for to in range(rights):
+            for band in range(bands):
+                top = to * out_y + band * BAND
+                for n in range(count):
+                    rows = pl.ds(pl.multiple_of((spot + n) * BAND, BAND), BAND)
+                    send_b[field, to, band, rows, :] = got[top:top + BAND, n * share_x:(n + 1) * share_x]
         for k in range(half):
-            @pl.when(jnp.logical_or(end, p < held))
+            @pl.when(jnp.logical_or(end, field < fields - 1))
             def _():
-                copy_b(p, crossing(k)).start()
+                copy_b(field, spot, count, crossing(k)).start()
         for k in range(half - 1):
-            copy_b(p, beside(k)).start()
-        spot = (lax.rem(i, pieces) * DEPTH + sub * SUB) * BAND
+            copy_b(field, spot, count, beside(k)).start()
         for band in range(bands):
-            mine = send_b[field, right, band, pl.ds(pl.multiple_of(spot, BAND), SUB * BAND), :]
-            there = pl.multiple_of(right * share_z * BAND + spot, BAND)
-            second[field, band, pl.ds(there, SUB * BAND), :] = mine
+            mine = send_b[field, right, band, pl.ds(pl.multiple_of(spot * BAND, BAND), count * BAND), :]
+            there = pl.multiple_of((right * share_z + spot) * BAND, BAND)
+            second[field, band, pl.ds(there, count * BAND), :] = mine
 
     fetch(1)
     tables[0].wait()
     tables[1].wait()
-    x_step(0, True)
+    x_open()
     tables[2].wait()
     tables[3].wait()
+    for z in range(SUB):
+        y_step(0, z, 1, rp_sem.at[z])
 
     def step(i, carry):
-        y_step(i, 0, i * subs)
-
         @pl.when(i + 1 < chunks)
         def _():
-            x_step(i + 1, False)
+            x_step(i + 1)
 
         def part(sub, carry):
-            y_step(i, sub, i * subs + sub)
+            y_step(i, sub * SUB, SUB, ra_sem.at[i, sub])
             return carry
 
         lax.fori_loop(1, subs, part, 0)
+
+        @pl.when(i + 1 < chunks)
+        def _():
+            y_step(i + 1, 0, SUB, ra_sem.at[i + 1, 0])
+
         return carry
 
     lax.fori_loop(0, chunks, step, 0)
 
     @pl.when(jnp.logical_not(end))
     def _():
-        for band in range(bands):
+        for n in range(2 * bands):
             for k in range(half):
-                copy_c(band, crossing(k)).start()
+                copy_c(n, crossing(k)).start()
+
+    for table in tables[4:]:
+        table.wait()
+    column = jnp.broadcast_to(sym_x[pl.ds(left, 1), :], (size_z, share_x)).T
+    base[...] = column + sym_z[...]
 
     def z_step(n, carry):
-        field, band = n // bands, lax.rem(n, bands)
-
+        field, part = n // (2 * bands), lax.rem(n, 2 * bands)
+        band, top = part // 2, lax.rem(part, 2) * SUBLANES
         for sources, chosen in ((rights - 1, field < fields - 1), (half, field == fields - 1)):
-            @pl.when(jnp.logical_and(band == 0, chosen))
+            @pl.when(jnp.logical_and(part == 0, chosen))
             def _():
                 landed(second.at[field, :, pl.ds(0, sources * share_z * BAND), :], rb_sem.at[field])
 
         @pl.when(field == fields - 1)
         def _():
-            landed(second.at[field, band, pl.ds(0, (half - 1) * share_z * BAND), :], rc_sem.at[band])
+            block = second.at[field, band].reshape(size_z, BAND, share_x)
+            landed(block.at[pl.ds(0, (half - 1) * share_z), pl.ds(top, SUBLANES), :], rc_sem.at[part])
 
         table = hz[...]
 
-        def line(y, carry):
+        def line(step, carry):
+            y = top + step
             plane = second[field, band, pl.ds(y, size_z, stride=BAND), :].T
             got = jnp.dot(jnp.concatenate(split(plane), axis=1), table, preferred_element_type=jnp.float32)
             got = (got[:, :size_z] + got[:, size_z:]) * lax.rsqrt(base[...] + sym_y[right * out_y + band * BAND + y])
             out[field, band, pl.ds(y, share_x, stride=BAND), :] = got
             return carry
 
-        lax.fori_loop(0, BAND, line, 0, unroll=4)
+        lax.fori_loop(0, SUBLANES, line, 0, unroll=4)
         return carry
 
-    lax.fori_loop(0, fields * bands, z_step, 0)
-
+    lax.fori_loop(0, fields * bands * 2, z_step, 0)
     landed(send_a.at[:, pl.ds(0, lefts - 1)], sa_sem)
     landed(send_b.at[:, pl.ds(0, rights - 1)], sb_sem)
 
@@ -519,7 +559,6 @@
     share_x, out_y = size_x // lefts, size_y // rights
     bands = out_y // BAND
     chunks = fields * (share_z // DEPTH)
-    parts = chunks * (DEPTH // SUB)
     data = jnp.transpose(tracer, (0, 2, 3, 1))
     low, high = factors_of(size_x)
     hy, hz = small_table(size_y), stacked(small_table(size_z))
@@ -531,7 +570,7 @@
         functools.partial(near_kernel, lefts, rights),
         name="modes",
         out_shape=pltpu.VMEM((fields, bands, share_x * BAND, size_z), f32),
-        in_specs=[*[any_space] * 5, vmem, vmem, pl.BlockSpec(memory_space=pltpu.SMEM)],
+        in_specs=[any_space] * 8,
         out_specs=vmem,
         scratch_shapes=[
             pltpu.VMEM((chunks, DEPTH, size_y, share_x), f32),
@@ -546,13 +585,17 @@
             pltpu.VMEM((chunks, lefts, DEPTH, share_y, share_x), f32),
             pltpu.VMEM((fields, rights, bands, share_z * BAND, share_x), f32),
             pltpu.VMEM((share_x, size_z), f32),
+            pltpu.VMEM((lefts, share_x), f32),
+            pltpu.VMEM((1, size_z), f32),
+            pltpu.SMEM((size_y,), f32),
             dma((2,)),
-            dma((4,)),
+            dma((7,)),
             dma,
             dma((chunks, DEPTH // SUB)),
+            dma((SUB,)),
             dma,
             dma((fields,)),
-            dma((bands,)),
+            dma((2 * bands,)),
         ],
         compiler_params=pltpu.CompilerParams(
             collective_id=0, has_side_effects=True, vmem_limit_bytes=NEAR_LIMIT

time: 199 us -> 197 us (0.990)
  Pallas kernels: 198 us -> 196 us
where the time goes in v3:
time: 197 us; the launch traced here: 196 us
  Pallas kernels  196 us (99%)
    pallas_call x1, Pallas kernels, near_local(): pl.pallas_call(functools.partial(near_kernel, lefts, rights), name='modes...  193 us

profile of v3, /device:TPU:0, one launch (start us, length us, event | category | flops | bytes accessed | tf_op | source)
XLA Modules:
  0.0 196.5 jit_solution(2876396085435054284)
XLA Ops:
  0.0 193.1 %modes.1 = f32[2,4,2048,128]{3,2,1,0:T(8,128)S(1)} custom-call(f32[2,32,32,1024]{3,2,1,0:T(8,128)} %bitcast.5, f32[2,32,1024]{2,1,0:T(8,128)} %constant.10.clone.low_in, f32[2,32,1024]{2,1,0:T(8,128)} %constant.11.clone.high_in, bf16[2,256,256]{2,1,0:T(8,128)(2,1)} %constant.12.clone.hy_in, bf16[256,256]{1,0:T(8,128)(2,1)} %constant.22.hz_in, ...), custom_call_target="tpu_custom_call" | custom-call | tf_op jit(solution)/shard_map/modes/pallas_call | solution.py:569
  193.1 3.3 %flush.1 = f32[2,128,64,128]{3,2,1,0:T(8,128)} custom-call(f32[2,4,128,16,128]{4,3,2,1,0:T(8,128)S(1)} %bitcast.4), custom_call_target="tpu_custom_call" | custom-call | tf_op jit(solution)/shard_map/flush/pallas_call | solution.py:604

commit v4 on v3

--- a/solution.py
+++ b/solution.py
@@ -280,7 +280,8 @@
 
 def near_kernel(lefts, rights, data, low_in, high_in, hy_in, hz_in, x_in, z_in, y_in, out, *rest):
     (first, second, dbuf, low, high, hx, hy, hz, lines, send_a, send_b, base,
-     sym_x, sym_z, sym_y, d_sem, t_sem, sa_sem, ra_sem, rp_sem, sb_sem, rb_sem, rc_sem) = rest
+     sym_x, sym_z, sym_y, raw_out, raw_in, guest_a, guest_first, guest_b,
+     d_sem, t_sem, sa_sem, ra_sem, rp_sem, sb_sem, rb_sem, rc_sem, raw_sem, guest_sem) = rest
     fields, share_y, share_z, size_x = data.shape
     size_y = hy.shape[1]
     share_x, size_z = base.shape
@@ -329,11 +330,11 @@
             device_id_type=MESH,
         )
 
-    def copy_b(field, spot, count, to):
+    def copy_b(field, spot, count, to, kind):
         return pltpu.make_async_remote_copy(
             src_ref=send_b.at[field, to, :, pl.ds(spot * BAND, count * BAND), :],
             dst_ref=second.at[field, :, pl.ds((right * share_z + spot) * BAND, count * BAND), :],
-            send_sem=sb_sem,
+            send_sem=sb_sem.at[jnp.where(field == 0, kind, 2)],
             recv_sem=rb_sem.at[field],
             device_id=(left, to),
             device_id_type=MESH,
@@ -345,7 +346,7 @@
         return pltpu.make_async_remote_copy(
             src_ref=send_b.at[fields - 1, to, band].reshape(share_z, BAND, share_x).at[:, rows, :],
             dst_ref=there.at[pl.ds(right * share_z, share_z), rows, :],
-            send_sem=sb_sem,
+            send_sem=sb_sem.at[2],
             recv_sem=rc_sem.at[n],
             device_id=(left, to),
             device_id_type=MESH,
@@ -354,6 +355,9 @@
     lower = right < half
     rank = jnp.where(lower, right, rights - 1 - right)
     end = rank == 0
+    gate = rank == half - 1
+    twin = rights - 1 - right
+    guest_z = DEPTH - SUB
 
     def mirrored(t):
         return jnp.where(lower, t, rights - 1 - t)
@@ -363,6 +367,37 @@
 
     def beside(k):
         return mirrored(lax.rem(rank + 1 + k, half))
+
+    def raw():
+        return pltpu.make_async_remote_copy(
+            src_ref=raw_out,
+            dst_ref=raw_in,
+            send_sem=raw_sem.at[0],
+            recv_sem=raw_sem.at[1],
+            device_id=(left, twin),
+            device_id_type=MESH,
+        )
+
+    def copy_guest_a(to):
+        return pltpu.make_async_remote_copy(
+            src_ref=guest_a.at[to],
+            dst_ref=guest_first.at[:, pl.ds(left * share_y, share_y), :],
+            send_sem=guest_sem.at[0],
+            recv_sem=guest_sem.at[1],
+            device_id=(to, right),
+            device_id_type=MESH,
+        )
+
+    def copy_guest_b(to):
+        spot = (twin * share_z + guest_z) * BAND
+        return pltpu.make_async_remote_copy(
+            src_ref=guest_b.at[to],
+            dst_ref=second.at[0, :, pl.ds(spot, SUB * BAND), :],
+            send_sem=guest_sem.at[2],
+            recv_sem=rb_sem.at[0],
+            device_id=(left, to),
+            device_id_type=MESH,
+        )
 
     def widen(cols):
         for top in range(size_x // low.shape[1]):
@@ -373,7 +408,7 @@
     def partner(k):
         return left ^ k if lefts & (lefts - 1) == 0 else lax.rem(left + k, lefts)
 
-    def x_tile(i, j, z, count, opening):
+    def x_tile(sends, j, z, count, opening):
         pair = partner(lefts - 1 - 2 * j) // 2
         cols = pl.ds(pl.multiple_of(pair * 2 * share_x, 2 * share_x), 2 * share_x)
         if opening:
@@ -382,7 +417,7 @@
         got = product((lines[0, rows, :], lines[1, rows, :]), (hx[0, :, cols], hx[1, :, cols]))
         for core in range(2):
             part = got[:, core * share_x:(core + 1) * share_x].reshape(count, share_y, share_x)
-            send_a[i, 2 * pair + core, z:z + count] = part
+            sends[2 * pair + core, z:z + count] = part
         return pair
 
     def x_split(i, planes):
@@ -411,12 +446,21 @@
     def x_open():
         landed(dbuf.at[0], d_sem.at[0])
         x_split(0, range(SUB))
-        pair = x_tile(0, 0, 0, SUB, True)
+        for c in range(size_x // LANES):
+            for z in range(SUB):
+                line = dbuf[0, c, pl.ds(guest_z + z, share_y, stride=DEPTH), :]
+                raw_out[z * share_y:(z + 1) * share_y, c * LANES:(c + 1) * LANES] = line
+        pair = x_tile(send_a.at[0], 0, 0, SUB, True)
         pl.semaphore_wait(barrier, lefts + rights - 2)
+
+        @pl.when(gate)
+        def _():
+            raw().start()
+
         x_send(0, 0, 1, pair, rp_sem.at[0])
 
         def tile(j, carry):
-            x_send(0, 0, 1, x_tile(0, j, 0, SUB, True), rp_sem.at[0])
+            x_send(0, 0, 1, x_tile(send_a.at[0], j, 0, SUB, True), rp_sem.at[0])
             return carry
 
         lax.fori_loop(1, lefts // 2, tile, 0)
@@ -427,7 +471,7 @@
         x_split(0, range(SUB, DEPTH))
 
         def more(j, carry):
-            x_send(0, SUB, SUB, x_tile(0, j, SUB, DEPTH - SUB, False), ra_sem.at[0, 1])
+            x_send(0, SUB, SUB, x_tile(send_a.at[0], j, SUB, DEPTH - SUB, False), ra_sem.at[0, 1])
             return carry
 
         lax.fori_loop(0, lefts // 2, more, 0)
@@ -445,34 +489,62 @@
             fetch(i + 2)
 
         def tile(j, carry):
-            x_send(i, 0, SUB, x_tile(i, j, 0, DEPTH, False), ra_sem.at[i, 0])
+            x_send(i, 0, SUB, x_tile(send_a.at[i], j, 0, DEPTH, False), ra_sem.at[i, 0])
             return carry
 
         lax.fori_loop(0, lefts // 2, tile, 0)
         x_rest(i, range(1, subs))
         x_own(i, 0, DEPTH)
 
-    def y_step(i, z, count, sem):
-        landed(first.at[i, pl.ds(z, count), pl.ds(0, (lefts - 1) * share_y), :], sem)
-        field, spot = i // pieces, lax.rem(i, pieces) * DEPTH + z
-        wide = jnp.concatenate([first[i, z + n] for n in range(count)], axis=1)
-        got = product((hy[0], hy[1]), split(wide))
+    def y_values(ready, sends, spot, count):
+        got = product((hy[0], hy[1]), split(jnp.concatenate([ready[n] for n in range(count)], axis=1)))
         for to in range(rights):
             for band in range(bands):
                 top = to * out_y + band * BAND
                 for n in range(count):
                     rows = pl.ds(pl.multiple_of((spot + n) * BAND, BAND), BAND)
-                    send_b[field, to, band, rows, :] = got[top:top + BAND, n * share_x:(n + 1) * share_x]
+                    sends[to, band, rows, :] = got[top:top + BAND, n * share_x:(n + 1) * share_x]
+
+    def y_own(sends, spot, field, there, count):
+        for band in range(bands):
+            mine = sends[right, band, pl.ds(pl.multiple_of(spot * BAND, BAND), count * BAND), :]
+            second[field, band, pl.ds(pl.multiple_of(there * BAND, BAND), count * BAND), :] = mine
+
+    def y_step(i, z, count, sem):
+        landed(first.at[i, pl.ds(z, count), pl.ds(0, (lefts - 1) * share_y), :], sem)
+        field, spot = i // pieces, lax.rem(i, pieces) * DEPTH + z
+        y_values(first.at[i, pl.ds(z, count)], send_b.at[field], spot, count)
+        hosted = jnp.logical_and(gate, jnp.logical_and(i == 0, z == guest_z))
+        direct = jnp.logical_or(end, jnp.logical_and(field < fields - 1, jnp.logical_not(hosted)))
         for k in range(half):
-            @pl.when(jnp.logical_or(end, field < fields - 1))
+            @pl.when(direct)
             def _():
-                copy_b(field, spot, count, crossing(k)).start()
+                copy_b(field, spot, count, crossing(k), 0).start()
         for k in range(half - 1):
-            copy_b(field, spot, count, beside(k)).start()
-        for band in range(bands):
-            mine = send_b[field, right, band, pl.ds(pl.multiple_of(spot * BAND, BAND), count * BAND), :]
-            there = pl.multiple_of((right * share_z + spot) * BAND, BAND)
-            second[field, band, pl.ds(there, count * BAND), :] = mine
+            copy_b(field, spot, count, beside(k), 1).start()
+        y_own(send_b.at[field], spot, field, right * share_z + spot, count)
+
+    def guest_x():
+        landed(raw_in, raw_sem.at[1])
+        for c in range(size_x // LANES):
+            cols = pl.ds(c * LANES, LANES)
+            lines[0, pl.ds(0, SUB * share_y), cols], lines[1, pl.ds(0, SUB * share_y), cols] = split(raw_in[:, cols])
+
+        def tile(j, carry):
+            x_tile(guest_a, j, 0, SUB, False)
+            return carry
+
+        lax.fori_loop(0, lefts // 2, tile, 0)
+        for k in range(lefts - 1, 0, -1):
+            copy_guest_a(partner(k)).start()
+        guest_first[:, pl.ds(pl.multiple_of(left * share_y, share_y), share_y), :] = guest_a[left]
+
+    def guest_y():
+        landed(guest_first.at[:, pl.ds(0, (lefts - 1) * share_y), :], guest_sem.at[1])
+        y_values(guest_first, guest_b, 0, SUB)
+        for k in range(half - 1):
+            copy_guest_b(beside(k)).start()
+        y_own(guest_b, 0, 0, twin * share_z + guest_z, SUB)
 
     fetch(1)
     tables[0].wait()
@@ -488,11 +560,19 @@
         def _():
             x_step(i + 1)
 
+        @pl.when(jnp.logical_and(gate, i == min(1, chunks - 1)))
+        def _():
+            guest_x()
+
         def part(sub, carry):
             y_step(i, sub * SUB, SUB, ra_sem.at[i, sub])
             return carry
 
         lax.fori_loop(1, subs, part, 0)
+
+        @pl.when(jnp.logical_and(gate, i == min(2, chunks - 1)))
+        def _():
+            guest_y()
 
         @pl.when(i + 1 < chunks)
         def _():
@@ -516,10 +596,16 @@
     def z_step(n, carry):
         field, part = n // (2 * bands), lax.rem(n, 2 * bands)
         band, top = part // 2, lax.rem(part, 2) * SUBLANES
-        for sources, chosen in ((rights - 1, field < fields - 1), (half, field == fields - 1)):
+        hosting = jnp.logical_and(gate, field == 0)
+        everything = (rights - 1) * share_z
+        for planes, chosen in (
+            (everything - SUB, hosting),
+            (everything, jnp.logical_and(field < fields - 1, jnp.logical_not(hosting))),
+            (half * share_z, field == fields - 1),
+        ):
             @pl.when(jnp.logical_and(part == 0, chosen))
             def _():
-                landed(second.at[field, :, pl.ds(0, sources * share_z * BAND), :], rb_sem.at[field])
+                landed(second.at[field, :, pl.ds(0, planes * BAND), :], rb_sem.at[field])
 
         @pl.when(field == fields - 1)
         def _():
@@ -541,7 +627,19 @@
 
     lax.fori_loop(0, fields * bands * 2, z_step, 0)
     landed(send_a.at[:, pl.ds(0, lefts - 1)], sa_sem)
-    landed(send_b.at[:, pl.ds(0, rights - 1)], sb_sem)
+    landed(send_b.at[0, pl.ds(0, half - 1)], sb_sem.at[1])
+    landed(send_b.at[pl.ds(1, fields - 1), pl.ds(0, rights - 1)], sb_sem.at[2])
+
+    @pl.when(gate)
+    def _():
+        landed(send_b.at[0, pl.ds(0, half), :, pl.ds(0, (share_z - SUB) * BAND), :], sb_sem.at[0])
+        landed(raw_out, raw_sem.at[0])
+        landed(guest_a.at[pl.ds(0, lefts - 1)], guest_sem.at[0])
+        landed(guest_b.at[pl.ds(0, half - 1)], guest_sem.at[2])
+
+    @pl.when(jnp.logical_not(gate))
+    def _():
+        landed(send_b.at[0, pl.ds(0, half)], sb_sem.at[0])
 
 
 def flush_kernel(ready, out, sem):
@@ -588,14 +686,21 @@
             pltpu.VMEM((lefts, share_x), f32),
             pltpu.VMEM((1, size_z), f32),
             pltpu.SMEM((size_y,), f32),
+            pltpu.VMEM((SUB * share_y, size_x), f32),
+            pltpu.VMEM((SUB * share_y, size_x), f32),
+            pltpu.VMEM((lefts, SUB, share_y, share_x), f32),
+            pltpu.VMEM((SUB, size_y, share_x), f32),
+            pltpu.VMEM((rights, bands, SUB * BAND, share_x), f32),
             dma((2,)),
             dma((7,)),
             dma,
             dma((chunks, DEPTH // SUB)),
             dma((SUB,)),
-            dma,
+            dma((3,)),
             dma((fields,)),
             dma((2 * bands,)),
+            dma((2,)),
+            dma((3,)),
         ],
         compiler_params=pltpu.CompilerParams(
             collective_id=0, has_side_effects=True, vmem_limit_bytes=NEAR_LIMIT
@@ -668,6 +773,7 @@
     size_z, share_x = symbol_z.shape[0], size_x // lefts
     size = 4 * math.prod(tracer.shape)
     fits = size <= NEAR_BYTES // 2 and share_x == LANES and size_z == LANES and rights % 2 == 0
+    fits = fits and rights > 2 and fields > 1
     run = near_local if fits else far_local
     return run(lefts, rights, tracer, symbol_x, symbol_y, symbol_z)
 

time: 197 us -> 195 us (0.990)
  no operation moved by 1% of the time
where the time goes in v4:
time: 195 us
  Pallas kernels  195 us (100%)
    pallas_call x1, Pallas kernels, near_local(): pl.pallas_call(functools.partial(near_kernel, lefts, rights), name='modes...  191 us

profile of v4, /device:TPU:0, one launch (start us, length us, event | category | flops | bytes accessed | tf_op | source)
XLA Modules:
  0.0 194.6 jit_solution(13766590195617237455)
XLA Ops:
  0.0 191.3 %modes.1 = f32[2,4,2048,128]{3,2,1,0:T(8,128)S(1)} custom-call(f32[2,32,32,1024]{3,2,1,0:T(8,128)} %bitcast.5, f32[2,32,1024]{2,1,0:T(8,128)} %constant.10.clone.low_in, f32[2,32,1024]{2,1,0:T(8,128)} %constant.11.clone.high_in, bf16[2,256,256]{2,1,0:T(8,128)(2,1)} %constant.12.clone.hy_in, bf16[256,256]{1,0:T(8,128)(2,1)} %constant.22.hz_in, ...), custom_call_target="tpu_custom_call" | custom-call | tf_op jit(solution)/shard_map/modes/pallas_call | solution.py:667
  191.3 3.3 %flush.1 = f32[2,128,64,128]{3,2,1,0:T(8,128)} custom-call(f32[2,4,128,16,128]{4,3,2,1,0:T(8,128)S(1)} %bitcast.4), custom_call_target="tpu_custom_call" | custom-call | tf_op jit(solution)/shard_map/flush/pallas_call | solution.py:709

commit v5 on v4

--- a/solution.py
+++ b/solution.py
@@ -49,9 +49,11 @@
     low = angle(np.arange(inner))
     high = angle(np.arange(outer) * inner)
     scale = count ** (-0.5)
-    low = jnp.asarray(np.stack([np.cos(low), np.sin(low)]), jnp.float32)
-    high = jnp.asarray(np.stack([np.cos(high) + np.sin(high), np.cos(high) - np.sin(high)]) * scale, jnp.float32)
-    return low, high
+    low = np.stack([np.cos(low), np.sin(low)])
+    high = np.stack([np.cos(high) + np.sin(high), np.cos(high) - np.sin(high)]) * scale
+    rows = max(inner, outer)
+    padded = [np.pad(part, ((0, 0), (0, rows - part.shape[1]), (0, 0))) for part in (low, high)]
+    return jnp.asarray(np.concatenate(padded), jnp.float32), inner
 
 
 def halves_of(table):
@@ -278,10 +280,10 @@
     )
 
 
-def near_kernel(lefts, rights, data, low_in, high_in, hy_in, hz_in, x_in, z_in, y_in, out, *rest):
-    (first, second, dbuf, low, high, hx, hy, hz, lines, send_a, send_b, base,
+def near_kernel(lefts, rights, inner, data, factors_in, hy_in, hz_in, x_in, z_in, y_in, out, tail, scale, table, *rest):
+    (first, second, dbuf, factors, hx, hy, hz, lines, send_a, send_b, base,
      sym_x, sym_z, sym_y, raw_out, raw_in, guest_a, guest_first, guest_b,
-     d_sem, t_sem, sa_sem, ra_sem, rp_sem, sb_sem, rb_sem, rc_sem, raw_sem, guest_sem) = rest
+     d_sem, t_sem, sa_sem, ra_sem, sb_sem, rb_sem, rc_sem, raw_sem, guest_sem) = rest
     fields, share_y, share_z, size_x = data.shape
     size_y = hy.shape[1]
     share_x, size_z = base.shape
@@ -306,13 +308,15 @@
         for copy in load(i):
             copy.start()
 
-    tables = [pltpu.make_async_copy(a, b, t_sem.at[n]) for n, (a, b) in enumerate(
-        [(low_in, low), (high_in, high), (hy_in, hy), (hz_in, hz), (x_in, sym_x), (z_in, sym_z), (y_in, sym_y)])]
+    def copies(pairs):
+        return [pltpu.make_async_copy(a, b, t_sem.at[n]) for n, (a, b) in enumerate(pairs)]
+
+    tables = copies([(factors_in, factors), (hy_in, hy), (hz_in, hz)])
+    symbols = copies([(x_in, sym_x), (z_in, sym_z), (y_in, sym_y)])
     tables[0].start()
+    fetch(0)
     tables[1].start()
-    fetch(0)
-    for table in tables[2:]:
-        table.start()
+    tables[2].start()
 
     barrier = pltpu.get_barrier_semaphore()
     for k in range(1, lefts):
@@ -400,10 +404,14 @@
         )
 
     def widen(cols):
-        for top in range(size_x // low.shape[1]):
-            made = low[0, :, cols] * high[0, top:top + 1, cols] + low[1, :, cols] * high[1, top:top + 1, cols]
-            rows = pl.ds(top * low.shape[1], low.shape[1])
+        for top in range(size_x // inner):
+            plus, minus = factors[2, top:top + 1, cols], factors[3, top:top + 1, cols]
+            made = factors[0, :inner, cols] * plus + factors[1, :inner, cols] * minus
+            rows = pl.ds(top * inner, inner)
             hx[0, rows, cols], hx[1, rows, cols] = split(made)
+
+    def arrival(i, sub):
+        return ra_sem.at[lax.rem(i, SLOTS), sub]
 
     def partner(k):
         return left ^ k if lefts & (lefts - 1) == 0 else lax.rem(left + k, lefts)
@@ -437,7 +445,7 @@
     def x_rest(i, subs_left):
         for sub in subs_left:
             for k in range(lefts - 1, 0, -1):
-                copy_a(i, sub * SUB, SUB, partner(k), ra_sem.at[i, sub]).start()
+                copy_a(i, sub * SUB, SUB, partner(k), arrival(i, sub)).start()
 
     def x_own(i, z, count):
         mine = pl.ds(pl.multiple_of(left * share_y, share_y), share_y)
@@ -457,21 +465,21 @@
         def _():
             raw().start()
 
-        x_send(0, 0, 1, pair, rp_sem.at[0])
+        x_send(0, 0, 1, pair, arrival(0, 0))
 
         def tile(j, carry):
-            x_send(0, 0, 1, x_tile(send_a.at[0], j, 0, SUB, True), rp_sem.at[0])
+            x_send(0, 0, 1, x_tile(send_a.at[0], j, 0, SUB, True), arrival(0, 0))
             return carry
 
         lax.fori_loop(1, lefts // 2, tile, 0)
         for z in range(1, SUB):
             for k in range(lefts - 1, 0, -1):
-                copy_a(0, z, 1, partner(k), rp_sem.at[z]).start()
+                copy_a(0, z, 1, partner(k), arrival(2 * z, 0)).start()
         x_own(0, 0, SUB)
         x_split(0, range(SUB, DEPTH))
 
         def more(j, carry):
-            x_send(0, SUB, SUB, x_tile(send_a.at[0], j, SUB, DEPTH - SUB, False), ra_sem.at[0, 1])
+            x_send(0, SUB, SUB, x_tile(send_a.at[0], j, SUB, DEPTH - SUB, False), arrival(0, 1))
             return carry
 
         lax.fori_loop(0, lefts // 2, more, 0)
@@ -489,7 +497,7 @@
             fetch(i + 2)
 
         def tile(j, carry):
-            x_send(i, 0, SUB, x_tile(send_a.at[i], j, 0, DEPTH, False), ra_sem.at[i, 0])
+            x_send(i, 0, SUB, x_tile(send_a.at[i], j, 0, DEPTH, False), arrival(i, 0))
             return carry
 
         lax.fori_loop(0, lefts // 2, tile, 0)
@@ -548,12 +556,13 @@
 
     fetch(1)
     tables[0].wait()
+    x_open()
     tables[1].wait()
-    x_open()
     tables[2].wait()
-    tables[3].wait()
+    for symbol in symbols:
+        symbol.start()
     for z in range(SUB):
-        y_step(0, z, 1, rp_sem.at[z])
+        y_step(0, z, 1, arrival(2 * z, 0))
 
     def step(i, carry):
         @pl.when(i + 1 < chunks)
@@ -565,7 +574,7 @@
             guest_x()
 
         def part(sub, carry):
-            y_step(i, sub * SUB, SUB, ra_sem.at[i, sub])
+            y_step(i, sub * SUB, SUB, arrival(i, sub))
             return carry
 
         lax.fori_loop(1, subs, part, 0)
@@ -576,7 +585,7 @@
 
         @pl.when(i + 1 < chunks)
         def _():
-            y_step(i + 1, 0, SUB, ra_sem.at[i + 1, 0])
+            y_step(i + 1, 0, SUB, arrival(i + 1, 0))
 
         return carry
 
@@ -588,10 +597,18 @@
             for k in range(half):
                 copy_c(n, crossing(k)).start()
 
-    for table in tables[4:]:
-        table.wait()
+    for symbol in symbols:
+        symbol.wait()
     column = jnp.broadcast_to(sym_x[pl.ds(left, 1), :], (size_z, share_x)).T
     base[...] = column + sym_z[...]
+    table[...] = hz[...]
+    for y in range(SUBLANES):
+        scale[y] = lax.rsqrt(base[...] + sym_y[right * out_y + out_y - SUBLANES + y])
+
+    def held_in(band, part):
+        block = second.at[fields - 1, band].reshape(size_z, BAND, share_x)
+        rows = pl.ds(part % 2 * SUBLANES, SUBLANES)
+        landed(block.at[pl.ds(0, (half - 1) * share_z), rows, :], rc_sem.at[part])
 
     def z_step(n, carry):
         field, part = n // (2 * bands), lax.rem(n, 2 * bands)
@@ -609,15 +626,12 @@
 
         @pl.when(field == fields - 1)
         def _():
-            block = second.at[field, band].reshape(size_z, BAND, share_x)
-            landed(block.at[pl.ds(0, (half - 1) * share_z), pl.ds(top, SUBLANES), :], rc_sem.at[part])
-
-        table = hz[...]
+            held_in(band, part)
 
         def line(step, carry):
             y = top + step
             plane = second[field, band, pl.ds(y, size_z, stride=BAND), :].T
-            got = jnp.dot(jnp.concatenate(split(plane), axis=1), table, preferred_element_type=jnp.float32)
+            got = jnp.dot(jnp.concatenate(split(plane), axis=1), hz[...], preferred_element_type=jnp.float32)
             got = (got[:, :size_z] + got[:, size_z:]) * lax.rsqrt(base[...] + sym_y[right * out_y + band * BAND + y])
             out[field, band, pl.ds(y, share_x, stride=BAND), :] = got
             return carry
@@ -625,7 +639,10 @@
         lax.fori_loop(0, SUBLANES, line, 0, unroll=4)
         return carry
 
-    lax.fori_loop(0, fields * bands * 2, z_step, 0)
+    lax.fori_loop(0, fields * bands * 2 - 1, z_step, 0)
+    held_in(bands - 1, 2 * bands - 1)
+    block = second.at[fields - 1, bands - 1].reshape(size_z, BAND, share_x)
+    tail[...] = block[:, BAND - SUBLANES:, :].reshape(size_z * SUBLANES, share_x)
     landed(send_a.at[:, pl.ds(0, lefts - 1)], sa_sem)
     landed(send_b.at[0, pl.ds(0, half - 1)], sb_sem.at[1])
     landed(send_b.at[pl.ds(1, fields - 1), pl.ds(0, rights - 1)], sb_sem.at[2])
@@ -642,12 +659,19 @@
         landed(send_b.at[0, pl.ds(0, half)], sb_sem.at[0])
 
 
-def flush_kernel(ready, out, sem):
-    fields, bands = ready.shape[:2]
+def flush_kernel(ready, tail, scale, table, out, made, sem):
+    fields, bands, share_x, _, size_z = ready.shape
     for n in range(fields * bands):
         field, band = n // bands, n % bands
-        there = out.at[field, :, pl.ds(band * BAND, BAND), :]
-        pltpu.make_async_copy(ready.at[field, band], there, sem).start()
+        rows = BAND if n < fields * bands - 1 else BAND - SUBLANES
+        there = out.at[field, :, pl.ds(band * BAND, rows), :]
+        pltpu.make_async_copy(ready.at[field, band, :, pl.ds(0, rows), :], there, sem).start()
+    for y in range(SUBLANES):
+        plane = tail[pl.ds(y, size_z, stride=SUBLANES), :].T
+        got = jnp.dot(jnp.concatenate(split(plane), axis=1), table[...], preferred_element_type=jnp.float32)
+        made[pl.ds(y, share_x, stride=SUBLANES), :] = (got[:, :size_z] + got[:, size_z:]) * scale[y]
+    there = out.at[fields - 1, :, pl.ds(bands * BAND - SUBLANES, SUBLANES), :]
+    pltpu.make_async_copy(made.reshape(share_x, SUBLANES, size_z), there, sem).start()
     landed(out, sem)
 
 
@@ -658,24 +682,28 @@
     bands = out_y // BAND
     chunks = fields * (share_z // DEPTH)
     data = jnp.transpose(tracer, (0, 2, 3, 1))
-    low, high = factors_of(size_x)
+    factors, inner = factors_of(size_x)
     hy, hz = small_table(size_y), stacked(small_table(size_z))
     f32, bf16 = jnp.float32, jnp.bfloat16
     any_space = pl.BlockSpec(memory_space=pl.ANY)
     vmem = pl.BlockSpec(memory_space=pltpu.VMEM)
     dma = pltpu.SemaphoreType.DMA
-    ready = pl.pallas_call(
-        functools.partial(near_kernel, lefts, rights),
+    ready, *others = pl.pallas_call(
+        functools.partial(near_kernel, lefts, rights, inner),
         name="modes",
-        out_shape=pltpu.VMEM((fields, bands, share_x * BAND, size_z), f32),
-        in_specs=[any_space] * 8,
-        out_specs=vmem,
+        out_shape=[
+            pltpu.VMEM((fields, bands, share_x * BAND, size_z), f32),
+            pltpu.VMEM((size_z * SUBLANES, share_x), f32),
+            pltpu.VMEM((SUBLANES, share_x, size_z), f32),
+            pltpu.VMEM(hz.shape, bf16),
+        ],
+        in_specs=[any_space] * 7,
+        out_specs=[vmem] * 4,
         scratch_shapes=[
             pltpu.VMEM((chunks, DEPTH, size_y, share_x), f32),
             pltpu.VMEM((fields, bands, size_z * BAND, share_x), f32),
             pltpu.VMEM((2, size_x // LANES, share_y * DEPTH, LANES), f32),
-            pltpu.VMEM(low.shape, f32),
-            pltpu.VMEM(high.shape, f32),
+            pltpu.VMEM(factors.shape, f32),
             pltpu.VMEM((2, size_x, size_x), bf16),
             pltpu.VMEM(hy.shape, bf16),
             pltpu.VMEM(hz.shape, bf16),
@@ -692,10 +720,9 @@
             pltpu.VMEM((SUB, size_y, share_x), f32),
             pltpu.VMEM((rights, bands, SUB * BAND, share_x), f32),
             dma((2,)),
-            dma((7,)),
+            dma((3,)),
             dma,
-            dma((chunks, DEPTH // SUB)),
-            dma((SUB,)),
+            dma((SLOTS, DEPTH // SUB)),
             dma((3,)),
             dma((fields,)),
             dma((2 * bands,)),
@@ -705,16 +732,16 @@
         compiler_params=pltpu.CompilerParams(
             collective_id=0, has_side_effects=True, vmem_limit_bytes=NEAR_LIMIT
         ),
-    )(data, low, high, hy, hz, symbol_x.reshape(lefts, share_x), symbol_z.reshape(1, size_z), symbol_y)
+    )(data, factors, hy, hz, symbol_x.reshape(lefts, share_x), symbol_z.reshape(1, size_z), symbol_y)
     return pl.pallas_call(
         flush_kernel,
         name="flush",
         out_shape=jax.ShapeDtypeStruct((fields, share_x, out_y, size_z), f32),
-        in_specs=[vmem],
+        in_specs=[vmem] * 4,
         out_specs=any_space,
-        scratch_shapes=[dma],
+        scratch_shapes=[pltpu.VMEM((share_x * SUBLANES, size_z), f32), dma],
         compiler_params=pltpu.CompilerParams(vmem_limit_bytes=2**21),
-    )(ready.reshape(fields, bands, share_x, BAND, size_z))
+    )(ready.reshape(fields, bands, share_x, BAND, size_z), *others)
 
 
 def far_local(lefts, rights, tracer, symbol_x, symbol_y, symbol_z):

time: 195 us -> 194 us (level)
  no operation moved by 1% of the time
where the time goes in v5:
time: 194 us
  Pallas kernels  194 us (100%)
    pallas_call x1, Pallas kernels, near_local(): pl.pallas_call(functools.partial(near_kernel, lefts, rights, inner), name...  190 us

profile of v5, /device:TPU:0, one launch (start us, length us, event | category | flops | bytes accessed | tf_op | source)
XLA Modules:
  0.0 193.9 jit_solution(2904385278912299868)
XLA Ops:
  0.0 190.4 %modes.1 = (f32[2,4,2048,128]{3,2,1,0:T(8,128)S(1)}, f32[1024,128]{1,0:T(8,128)S(1)}, f32[8,128,128]{2,1,0:T(8,128)S(1)}, bf16[256,256]{1,0:T(8,128)(2,1)S(1)}) custom-call(f32[2,32,32,1024]{3,2,1,0:T(8,128)} %bitcast.5, f32[4,32,1024]{2,1,0:T(8,128)} %constant.8.clone.factors_in, bf16[2,256,256]{2,1,0:T(8,128)(2,1)} %constant.9.clone.hy_in, ...), custom_call_target="tpu_custom_call" | custom-call | tf_op jit(solution)/shard_map/modes/pallas_call | solution.py:691
  190.5 3.4 %flush.1 = f32[2,128,64,128]{3,2,1,0:T(8,128)} custom-call(f32[2,4,128,16,128]{4,3,2,1,0:T(8,128)S(1)} %bitcast.4, f32[1024,128]{1,0:T(8,128)S(1)} %get-tuple-element.10.tail, f32[8,128,128]{2,1,0:T(8,128)S(1)} %get-tuple-element.11.scale, bf16[256,256]{1,0:T(8,128)(2,1)S(1)} %get-tuple-element.12.table), custom_call_target="tpu_custom_call" | custom-call | tf_op jit(solution)/shard_map/flush/pallas_call | solution.py:736

commit v6 on v5

--- a/solution.py
+++ b/solution.py
@@ -594,7 +594,7 @@
     @pl.when(jnp.logical_not(end))
     def _():
         for n in range(2 * bands):
-            for k in range(half):
+            for k in range(half - 1, -1, -1):
                 copy_c(n, crossing(k)).start()
 
     for symbol in symbols:

time: 194 us -> 192 us (0.990)
  Pallas kernels: 194 us -> 192 us
    pallas_call x1, Pallas kernels: 190 us -> 188 us  [near_local(): pl.pallas_call(functools.partial(near_kernel, lefts, rights, inner), name...]
where the time goes in v6:
time: 192 us
  Pallas kernels  192 us (100%)
    pallas_call x1, Pallas kernels, near_local(): pl.pallas_call(functools.partial(near_kernel, lefts, rights, inner), name...  188 us

profile of v6, /device:TPU:0, one launch (start us, length us, event | category | flops | bytes accessed | tf_op | source)
XLA Modules:
  0.0 191.6 jit_solution(3037270469073122676)
XLA Ops:
  0.0 188.2 %modes.1 = (f32[2,4,2048,128]{3,2,1,0:T(8,128)S(1)}, f32[1024,128]{1,0:T(8,128)S(1)}, f32[8,128,128]{2,1,0:T(8,128)S(1)}, bf16[256,256]{1,0:T(8,128)(2,1)S(1)}) custom-call(f32[2,32,32,1024]{3,2,1,0:T(8,128)} %bitcast.5, f32[4,32,1024]{2,1,0:T(8,128)} %constant.8.clone.factors_in, bf16[2,256,256]{2,1,0:T(8,128)(2,1)} %constant.9.clone.hy_in, ...), custom_call_target="tpu_custom_call" | custom-call | tf_op jit(solution)/shard_map/modes/pallas_call | solution.py:691
  188.2 3.4 %flush.1 = f32[2,128,64,128]{3,2,1,0:T(8,128)} custom-call(f32[2,4,128,16,128]{4,3,2,1,0:T(8,128)S(1)} %bitcast.4, f32[1024,128]{1,0:T(8,128)S(1)} %get-tuple-element.10.tail, f32[8,128,128]{2,1,0:T(8,128)S(1)} %get-tuple-element.11.scale, bf16[256,256]{1,0:T(8,128)(2,1)S(1)} %get-tuple-element.12.table), custom_call_target="tpu_custom_call" | custom-call | tf_op jit(solution)/shard_map/flush/pallas_call | solution.py:736

commit v7 on v6

--- a/solution.py
+++ b/solution.py
@@ -313,16 +313,16 @@
 
     tables = copies([(factors_in, factors), (hy_in, hy), (hz_in, hz)])
     symbols = copies([(x_in, sym_x), (z_in, sym_z), (y_in, sym_y)])
-    tables[0].start()
-    fetch(0)
-    tables[1].start()
-    tables[2].start()
-
     barrier = pltpu.get_barrier_semaphore()
     for k in range(1, lefts):
         pl.semaphore_signal(barrier, inc=1, device_id=(lax.rem(left + k, lefts), right), device_id_type=MESH)
     for k in range(1, rights):
         pl.semaphore_signal(barrier, inc=1, device_id=(left, lax.rem(right + k, rights)), device_id_type=MESH)
+
+    tables[0].start()
+    fetch(0)
+    tables[1].start()
+    tables[2].start()
 
     def copy_a(i, z, count, to, sem):
         return pltpu.make_async_remote_copy(
@@ -453,18 +453,18 @@
 
     def x_open():
         landed(dbuf.at[0], d_sem.at[0])
-        x_split(0, range(SUB))
         for c in range(size_x // LANES):
             for z in range(SUB):
                 line = dbuf[0, c, pl.ds(guest_z + z, share_y, stride=DEPTH), :]
                 raw_out[z * share_y:(z + 1) * share_y, c * LANES:(c + 1) * LANES] = line
+        x_split(0, range(SUB))
+        pl.semaphore_wait(barrier, lefts + rights - 2)
+
+        @pl.when(gate)
+        def _():
+            raw().start()
+
         pair = x_tile(send_a.at[0], 0, 0, SUB, True)
-        pl.semaphore_wait(barrier, lefts + rights - 2)
-
-        @pl.when(gate)
-        def _():
-            raw().start()
-
         x_send(0, 0, 1, pair, arrival(0, 0))
 
         def tile(j, carry):
@@ -529,7 +529,9 @@
             def _():
                 copy_b(field, spot, count, crossing(k), 0).start()
         for k in range(half - 1):
-            copy_b(field, spot, count, beside(k), 1).start()
+            @pl.when(jnp.logical_not(field == fields - 1))
+            def _():
+                copy_b(field, spot, count, beside(k), 1).start()
         y_own(send_b.at[field], spot, field, right * share_z + spot, count)
 
     def guest_x():
@@ -590,6 +592,9 @@
         return carry
 
     lax.fori_loop(0, chunks, step, 0)
+
+    for k in range(half - 1):
+        copy_b(fields - 1, 0, share_z, beside(k), 1).start()
 
     @pl.when(jnp.logical_not(end))
     def _():

time: 192 us -> 192 us (level)
  no operation moved by 1% of the time
where the time goes in v7:
time: 192 us
  Pallas kernels  192 us (100%)
    pallas_call x1, Pallas kernels, near_local(): pl.pallas_call(functools.partial(near_kernel, lefts, rights, inner), name...  188 us

profile of v7, /device:TPU:0, one launch (start us, length us, event | category | flops | bytes accessed | tf_op | source)
XLA Modules:
  0.0 191.6 jit_solution(9331940438080225027)
XLA Ops:
  0.0 188.2 %modes.1 = (f32[2,4,2048,128]{3,2,1,0:T(8,128)S(1)}, f32[1024,128]{1,0:T(8,128)S(1)}, f32[8,128,128]{2,1,0:T(8,128)S(1)}, bf16[256,256]{1,0:T(8,128)(2,1)S(1)}) custom-call(f32[2,32,32,1024]{3,2,1,0:T(8,128)} %bitcast.5, f32[4,32,1024]{2,1,0:T(8,128)} %constant.8.clone.factors_in, bf16[2,256,256]{2,1,0:T(8,128)(2,1)} %constant.9.clone.hy_in, ...), custom_call_target="tpu_custom_call" | custom-call | tf_op jit(solution)/shard_map/modes/pallas_call | solution.py:696
  188.2 3.4 %flush.1 = f32[2,128,64,128]{3,2,1,0:T(8,128)} custom-call(f32[2,4,128,16,128]{4,3,2,1,0:T(8,128)S(1)} %bitcast.4, f32[1024,128]{1,0:T(8,128)S(1)} %get-tuple-element.10.tail, f32[8,128,128]{2,1,0:T(8,128)S(1)} %get-tuple-element.11.scale, bf16[256,256]{1,0:T(8,128)(2,1)S(1)} %get-tuple-element.12.table), custom_call_target="tpu_custom_call" | custom-call | tf_op jit(solution)/shard_map/flush/pallas_call | solution.py:741

commit v8 on v7

--- a/solution.py
+++ b/solution.py
@@ -598,9 +598,10 @@
 
     @pl.when(jnp.logical_not(end))
     def _():
-        for n in range(2 * bands):
+        for parts in (*((n,) for n in range(2 * bands - 2)), (2 * bands - 2, 2 * bands - 1)):
             for k in range(half - 1, -1, -1):
-                copy_c(n, crossing(k)).start()
+                for n in parts:
+                    copy_c(n, crossing(k)).start()
 
     for symbol in symbols:
         symbol.wait()

time: 192 us -> 192 us (level); the launches traced: 192 us -> 189 us
  Pallas kernels: 192 us -> 189 us
    pallas_call x1, Pallas kernels: 188 us -> 185 us  [near_local(): pl.pallas_call(functools.partial(near_kernel, lefts, rights, inner), name...]
where the time goes in v8:
time: 192 us; the launch traced here: 189 us
  Pallas kernels  189 us (98%)
    pallas_call x1, Pallas kernels, near_local(): pl.pallas_call(functools.partial(near_kernel, lefts, rights, inner), name...  185 us

profile of v8, /device:TPU:0, one launch (start us, length us, event | category | flops | bytes accessed | tf_op | source)
XLA Modules:
  0.0 188.8 jit_solution(2691120219011788726)
XLA Ops:
  0.0 185.4 %modes.1 = (f32[2,4,2048,128]{3,2,1,0:T(8,128)S(1)}, f32[1024,128]{1,0:T(8,128)S(1)}, f32[8,128,128]{2,1,0:T(8,128)S(1)}, bf16[256,256]{1,0:T(8,128)(2,1)S(1)}) custom-call(f32[2,32,32,1024]{3,2,1,0:T(8,128)} %bitcast.5, f32[4,32,1024]{2,1,0:T(8,128)} %constant.8.clone.factors_in, bf16[2,256,256]{2,1,0:T(8,128)(2,1)} %constant.9.clone.hy_in, ...), custom_call_target="tpu_custom_call" | custom-call | tf_op jit(solution)/shard_map/modes/pallas_call | solution.py:697
  185.4 3.4 %flush.1 = f32[2,128,64,128]{3,2,1,0:T(8,128)} custom-call(f32[2,4,128,16,128]{4,3,2,1,0:T(8,128)S(1)} %bitcast.4, f32[1024,128]{1,0:T(8,128)S(1)} %get-tuple-element.10.tail, f32[8,128,128]{2,1,0:T(8,128)S(1)} %get-tuple-element.11.scale, bf16[256,256]{1,0:T(8,128)(2,1)S(1)} %get-tuple-element.12.table), custom_call_target="tpu_custom_call" | custom-call | tf_op jit(solution)/shard_map/flush/pallas_call | solution.py:742

commit v9 on v8

--- a/solution.py
+++ b/solution.py
@@ -565,6 +565,7 @@
         symbol.start()
     for z in range(SUB):
         y_step(0, z, 1, arrival(2 * z, 0))
+    y_step(0, SUB, SUB, arrival(0, 1))
 
     def step(i, carry):
         @pl.when(i + 1 < chunks)
@@ -579,7 +580,7 @@
             y_step(i, sub * SUB, SUB, arrival(i, sub))
             return carry
 
-        lax.fori_loop(1, subs, part, 0)
+        lax.fori_loop(jnp.where(i == 0, 2, 1), subs, part, 0)
 
         @pl.when(jnp.logical_and(gate, i == min(2, chunks - 1)))
         def _():

time: 192 us -> 192 us (level)
  no operation moved by 1% of the time
where the time goes in v9:
time: 192 us; the launch traced here: 189 us
  Pallas kernels  189 us (98%)
    pallas_call x1, Pallas kernels, near_local(): pl.pallas_call(functools.partial(near_kernel, lefts, rights, inner), name...  185 us

profile of v9, /device:TPU:0, one launch (start us, length us, event | category | flops | bytes accessed | tf_op | source)
XLA Modules:
  0.0 188.8 jit_solution(12230689878489982634)
XLA Ops:
  0.0 185.4 %modes.1 = (f32[2,4,2048,128]{3,2,1,0:T(8,128)S(1)}, f32[1024,128]{1,0:T(8,128)S(1)}, f32[8,128,128]{2,1,0:T(8,128)S(1)}, bf16[256,256]{1,0:T(8,128)(2,1)S(1)}) custom-call(f32[2,32,32,1024]{3,2,1,0:T(8,128)} %bitcast.5, f32[4,32,1024]{2,1,0:T(8,128)} %constant.8.clone.factors_in, bf16[2,256,256]{2,1,0:T(8,128)(2,1)} %constant.9.clone.hy_in, ...), custom_call_target="tpu_custom_call" | custom-call | tf_op jit(solution)/shard_map/modes/pallas_call | solution.py:698
  185.4 3.4 %flush.1 = f32[2,128,64,128]{3,2,1,0:T(8,128)} custom-call(f32[2,4,128,16,128]{4,3,2,1,0:T(8,128)S(1)} %bitcast.4, f32[1024,128]{1,0:T(8,128)S(1)} %get-tuple-element.10.tail, f32[8,128,128]{2,1,0:T(8,128)S(1)} %get-tuple-element.11.scale, bf16[256,256]{1,0:T(8,128)(2,1)S(1)} %get-tuple-element.12.table), custom_call_target="tpu_custom_call" | custom-call | tf_op jit(solution)/shard_map/flush/pallas_call | solution.py:743
